TPU v7x, 32 devices: a whole 2x2x4 slice. The times are simulated.
32 devices in a mesh: elem: 8 (over z, x), blk: 4 (over y, core).
Axes of the slice: x: 2, y: 2, z: 4, core: 2. Of those that a mesh axis runs over, the one named last changes fastest.
Arguments:
- diagonal_block_list: bfloat16 [32, 512, 512], P('elem', None, 'blk'), may hold values from -0.25 to 0.25
- neighbour_block_list: bfloat16 [32, 6, 512, 512], P('elem', None, None, 'blk'), may hold values from -0.25 to 0.25
- neighbours: int32 [32, 6], P('elem'), may hold values from 0 to 31, as said below
- damping: float32 [32, 512], P('elem', 'blk'), may hold values from 0.05 to 0.3
- bases: bfloat16 [32, 512, 128], P('elem', 'blk'), may hold values from -1.1953125 to 1.1953125
- agglomerate: int32 [32], replicated, may hold values from 0 to 15, as said below
- group: int32 [16], replicated, may hold values from 0 to 7
Outputs:
- smoothed: bfloat16 [32, 512, 128], P('elem', 'blk')
- coarse: float32 [16, 128, 128], P('elem', 'blk')
- last_level: float32 [8, 128, 128], P(None, 'blk')
Inputs may be any that keep to these rules, and one draw needn't show every extreme that they name: `neighbours`: each neighbour lies on the same index of elem as its element or on the next index on either side; every index of elem has a neighbour on an adjacent index. The elements of one agglomerate are consecutive; every agglomerate has one element or more.
All inputs are finite; a program needn't handle non-finite values.
Results may differ from a plain program's by a relative error of at most 0.007.
Values may be sent and summed in bfloat16 or wider, within the bound.
No kernel may reach another device: no remote copies, remote signals or barrier semaphores. Data moves between devices by JAX's collectives and lax.ppermute only.
A program may use at most 64 MiB of HBM per device.

v0:
```python
import jax
import jax.numpy as jnp
from jax import lax
from jax.sharding import PartitionSpec as P

SWEEPS = 2
NG = 8


def extended(x, sides, width):
    for axis, dim in sides:
        size, length = (lax.axis_size(axis), x.shape[dim])
        up = [(i, (i + 1) % size) for i in range(size - 1)]
        down = [(j, i) for i, j in up]
        last = lax.slice_in_dim(x, length - width, length, axis=dim)
        initial = lax.slice_in_dim(x, 0, width, axis=dim)
        before = lax.ppermute(last, axis, up)
        after = lax.ppermute(initial, axis, down)
        x = jnp.concatenate([before, x, after], axis=dim)
    return x


def nearby_slabs(slab, neighbour_ids, first_element):
    local_count = slab.shape[0]
    padded = extended(slab, (("elem", 0),), local_count)
    offsets = neighbour_ids - (first_element - local_count)
    return jnp.take(padded, offsets, axis=0)


def lookup_table(indices, table):
    positions = jnp.arange(table.shape[0], dtype=jnp.int32)
    matches = indices[..., None] == positions
    return jnp.sum(jnp.where(matches, table, 0), -1)


def body(diagonal_block_list, neighbour_block_list, neighbours, damping, bases, agglomerate, group):
    local_count = bases.shape[0]
    slab_rows = bases.shape[1]
    coarse_width = bases.shape[2]
    position = lax.axis_index("elem")
    first_element = position * local_count
    present_value = bases
    for sweep_index in range(SWEEPS):
        nearby_elements = nearby_slabs(present_value, neighbours, first_element)
        total_result = jnp.einsum(
            "dag,dgb->adb", diagonal_block_list, present_value, preferred_element_type=jnp.float32
        )
        total_result = total_result + jnp.einsum(
            "psgw,pswj->gpj",
            neighbour_block_list,
            nearby_elements,
            preferred_element_type=jnp.float32,
        )
        summed = lax.psum_scatter(
            total_result.reshape(lax.axis_size("blk") * slab_rows, local_count * coarse_width),
            "blk",
            scatter_dimension=0,
            tiled=True,
        )
        summed = summed.reshape(slab_rows, local_count, coarse_width).transpose(1, 0, 2)
        present_value = (present_value.astype(jnp.float32) - damping[:, :, None] * summed).astype(
            jnp.bfloat16
        )
    piece = lax.all_gather(present_value, "blk", axis=1, tiled=True)
    diag_left = jnp.einsum(
        "eic,eis->ecs", piece, diagonal_block_list, preferred_element_type=jnp.float32
    )
    nbr_left = jnp.einsum(
        "eic,ekis->ekcs", piece, neighbour_block_list, preferred_element_type=jnp.float32
    )
    diag_left, nbr_left = (diag_left, nbr_left)
    diag_left = diag_left.astype(jnp.bfloat16)
    nbr_left = nbr_left.astype(jnp.bfloat16)
    nearby_elements = nearby_slabs(present_value, neighbours, first_element)
    self_terms = jnp.einsum(
        "ecs,esd->ecd", diag_left, present_value, preferred_element_type=jnp.float32
    )
    nbr_terms = jnp.einsum(
        "ekcs,eksd->ekcd", nbr_left, nearby_elements, preferred_element_type=jnp.float32
    )
    own_cluster = lax.dynamic_slice_in_dim(agglomerate, first_element, local_count)
    nbr_agg = lookup_table(neighbours, agglomerate)
    own_group = lookup_table(own_cluster, group)
    nbr_group = lookup_table(nbr_agg, group)
    same_cluster = (nbr_agg == own_cluster[:, None]).astype(jnp.float32)
    same_group = (nbr_group == own_group[:, None]).astype(jnp.float32)
    first_sum = self_terms + jnp.sum(same_cluster[:, :, None, None] * nbr_terms, 1)
    second_level_sum = self_terms + jnp.sum(same_group[:, :, None, None] * nbr_terms, 1)
    first_rows, second_rows = (
        lax.psum_scatter(
            first_sum.astype(jnp.bfloat16), "blk", scatter_dimension=1, tiled=True
        ).astype(jnp.float32),
        lax.psum_scatter(
            second_level_sum.astype(jnp.bfloat16), "blk", scatter_dimension=1, tiled=True
        ).astype(jnp.float32),
    )
    owned_count = local_count // 2
    coarse_rows_count = first_rows.shape[1]
    owned_ids = position * owned_count + jnp.arange(owned_count, dtype=jnp.int32)
    empty_owned = jnp.zeros((owned_count, coarse_rows_count, coarse_width), jnp.float32)
    select = (agglomerate[:, None] == owned_ids[None, :]).astype(jnp.float32)
    coarse = empty_owned + jnp.einsum(
        "ra,rcd->acd",
        select,
        lax.all_gather(first_rows.astype(jnp.bfloat16), "elem", axis=0, tiled=True).astype(
            jnp.float32
        ),
        precision=lax.Precision.HIGHEST,
    )
    group_select = (own_group[:, None] == jnp.arange(NG, dtype=jnp.int32)[None, :]).astype(
        jnp.float32
    )
    level_terms = jnp.einsum(
        "eg,ecd->gcd", group_select, second_rows, precision=lax.Precision.HIGHEST
    )
    last_level = lax.psum(level_terms, "elem")
    return (present_value, coarse, last_level)


def solution(mesh):
    return jax.shard_map(
        body,
        mesh=mesh,
        in_specs=(
            P("elem", None, "blk"),
            P("elem", None, None, "blk"),
            P("elem", None),
            P("elem", "blk"),
            P("elem", "blk", None),
            P(),
            P(),
        ),
        out_specs=(P("elem", "blk", None), P("elem", "blk", None), P(None, "blk", None)),
        check_vma=False,
    )
```

profile of v0, /device:TPU:0, one launch (start us, length us, event | category | flops | bytes accessed | tf_op | source)
XLA Modules:
  0.0 244.1 jit_solution(7584779660295305088)
XLA Ops:
  7.2 5.1 %collective-permute-start = (bf16[4,128,128]{2,1,0:T(8,128)(2,1)}, bf16[4,128,128]{2,1,0:T(8,128)(2,1)S(1)}, u32[]{:S(2)}, u32[]{:S(2)}) collective-permute-start(bf16[4,128,128]{2,1,0:T(8,128)(2,1)} %param.13), channel_id=1, source_target_pairs={{0,4},{4,8},{8,12},{12,16},{16,20},{20,24},{24,28},{1,5},{5,9},{9,... | collective-permute-start | bytes 393224 | tf_op jit(solution)/shard_map/ppermute | solution.py:17
  12.4 1.3 collective-permute-start.1
  13.7 0.7 compare_and_fusion
  14.4 0.1 reshape.102
  14.5 1.0 collective-permute-done
  15.4 0.7 copy-done.8
  16.1 3.5 %collective-permute-done.1 = bf16[4,128,128]{2,1,0:T(8,128)(2,1)} collective-permute-done((bf16[4,128,128]{2,1,0:T(8,128)(2,1)}, bf16[4,128,128]{2,1,0:T(8,128)(2,1)}, u32[]{:S(2)}, u32[]{:S(2)}) %collective-permute-start.1) | collective-permute-done | bytes 131104 | tf_op jit(solution)/shard_map/ppermute | solution.py:18
  19.6 1.1 pad_maximum_fusion
  20.6 1.6 gather_fusion
  22.2 2.3 copy.40
  24.5 2.3 convolution_bitcast_fusion.1
  26.9 1.3 convolution_add_fusion.1
  28.3 0.1 copy.38
  28.4 26.0 %reduce-scatter.5.cloned.1.call-done = f32[128,512]{0,1:T(8,128)} async-done(((f32[512,512]{0,1:T(8,128)}), f32[128,512]{0,1:T(8,128)}) %reduce-scatter.5.cloned.1.call-update) | async-done | bytes 262160 | tf_op jit(solution)/shard_map/reduce_scatter | solution.py:54
  54.4 1.0 subtract_convert_fusion.1
  55.4 3.4 %collective-permute-start.2 = (bf16[4,128,128]{1,2,0:T(8,128)(2,1)S(1)}, bf16[4,128,128]{1,2,0:T(8,128)(2,1)S(1)}, u32[]{:S(2)}, u32[]{:S(2)}) collective-permute-start(bf16[4,128,128]{1,2,0:T(8,128)(2,1)S(1)} %subtract_convert_fusion.1), channel_id=1, source_target_pairs={{0,4},{4,8},{8,12},{12,16},{16,20},{20,24},{24,28},{1,5},{5,9},{9,... | collective-permute-start | bytes 393224 | tf_op jit(solution)/shard_map/ppermute | solution.py:17
  58.8 1.3 collective-permute-start.3
  60.1 1.3 collective-permute-done.2
  61.4 4.3 %collective-permute-done.3 = bf16[4,128,128]{1,2,0:T(8,128)(2,1)S(1)} collective-permute-done((bf16[4,128,128]{1,2,0:T(8,128)(2,1)S(1)}, bf16[4,128,128]{1,2,0:T(8,128)(2,1)S(1)}, u32[]{:S(2)}, u32[]{:S(2)}) %collective-permute-start.3) | collective-permute-done | bytes 131104 | tf_op jit(solution)/shard_map/ppermute | solution.py:18
  65.7 1.6 gather_fusion.1
  67.3 2.3 convolution_bitcast_fusion
  69.7 1.3 convolution_add_fusion
  71.0 0.1 copy.42
  71.1 0.1 dynamic_slice.3
  71.2 0.2 select_reduce_fusion.2
  71.4 0.2 select_reduce_fusion.1
  71.6 0.3 select_reduce_fusion
  71.9 0.7 copy.46
  72.6 0.7 copy.43
  73.3 22.7 %reduce-scatter.7.cloned.1.call-done = f32[128,512]{0,1:T(8,128)} async-done(((f32[512,512]{0,1:T(8,128)}), f32[128,512]{0,1:T(8,128)}) %reduce-scatter.7.cloned.1.call-update) | async-done | bytes 262160 | tf_op jit(solution)/shard_map/reduce_scatter | solution.py:54
  95.9 1.0 subtract_convert_fusion
  96.9 3.5 %collective-permute-start.4 = (bf16[4,128,128]{1,2,0:T(8,128)(2,1)S(1)}, bf16[4,128,128]{1,2,0:T(8,128)(2,1)S(1)}, u32[]{:S(2)}, u32[]{:S(2)}) collective-permute-start(bf16[4,128,128]{1,2,0:T(8,128)(2,1)S(1)} %subtract_convert_fusion), channel_id=1, source_target_pairs={{0,4},{4,8},{8,12},{12,16},{16,20},{20,24},{24,28},{1,5},{5,9},{9,... | collective-permute-start | bytes 393224 | tf_op jit(solution)/shard_map/ppermute | solution.py:17
  100.5 1.3 collective-permute-start.5
  101.8 7.0 %all_gather.6 = bf16[4,512,128]{1,2,0:T(8,128)(2,1)} all-gather(bf16[4,128,128]{1,2,0:T(8,128)(2,1)S(1)} %subtract_convert_fusion), channel_id=1, replica_groups=mesh['elem'=8,'blk'=4] {'blk'}, dimensions={1}, use_global_device_ids=true | all-gather | bytes 655360 | tf_op jit(solution)/shard_map/all_gather | solution.py:64
  108.8 1.6 gather_fusion.2
  110.4 2.3 copy.44
  112.7 2.9 %multiply_reduce_fusion = (f32[4,128,128]{2,1,0:T(8,128)S(1)}, f32[4,128,128]{2,1,0:T(8,128)}) fusion(f32[4,6]{1,0:T(4,128)S(1)} %copy-done.14, f32[4,6]{1,0:T(4,128)} %copy.43, bf16[4,6,128,128]{3,2,1,0:T(8,128)(2,1)} %copy.44, pred[4,6]{1,0:T(4,128)(4,1)S(1)} %get-tuple-element.18, bf16[4,6,512,128]{3,2,1,0:T(8,128)(2,1)S(1)} %copy-done, ...), kind=kOutput, calls=%fused_computation.3 | convolution fusion | flops 505544704 | bytes 4980952 | tf_op jit(solution)/shard_map/ekcs,eksd->ekcd/dot_general | solution.py:78
  115.6 2.4 add_convert_fusion
  118.1 0.5 reduce-scatter.9.cloned.1.call-update
  118.7 0.8 copy.48
  119.4 20.2 %reduce-scatter.11.cloned.1.call-done = bf16[4,32,128]{2,1,0:T(8,128)(2,1)} async-done(((bf16[4,128,128]{2,1,0:T(8,128)(2,1)}), bf16[4,32,128]{2,1,0:T(8,128)(2,1)}) %reduce-scatter.11.cloned.1.call-update) | async-done | bytes 32784 | tf_op jit(solution)/shard_map/reduce_scatter | solution.py:93
  139.7 1.7 fusion.16
  141.4 20.2 %reduce-scatter.9.cloned.1.call-done = bf16[4,32,128]{2,1,0:T(8,128)(2,1)} async-done(((bf16[4,128,128]{2,1,0:T(8,128)(2,1)}), bf16[4,32,128]{2,1,0:T(8,128)(2,1)}) %reduce-scatter.9.cloned.1.call-update) | async-done | bytes 32784 | tf_op jit(solution)/shard_map/reduce_scatter | solution.py:90
  161.6 31.1 %all_gather.7 = bf16[32,32,128]{2,1,0:T(8,128)(2,1)S(1)} all-gather(bf16[4,32,128]{2,1,0:T(8,128)(2,1)} %reduce-scatter.9.cloned.1.call-done), channel_id=1, replica_groups=mesh['elem'=8,'blk'=4] {'elem'}, dimensions={0}, use_global_device_ids=true | all-gather | bytes 294912 | tf_op jit(solution)/shard_map/all_gather | solution.py:105
  192.7 0.2 fusion.14
  192.9 0.6 copy.49
  193.6 42.4 %all-reduce.2.cloned.1.call-done = f32[8,32,128]{2,0,1:T(8,128)} async-done(((f32[8,32,128]{2,0,1:T(8,128)}), f32[8,32,128]{2,0,1:T(8,128)}) %all-reduce.2.cloned.1.call-update) | async-done | bytes 131088 | tf_op jit(solution)/shard_map/psum | solution.py:116
  236.0 1.6 copy.50
  (48 shorter events, 0.5 us)
Async XLA Ops:
  7.2 17.4 %copy-start = (bf16[4,6,512,128]{3,2,1,0:T(8,128)(2,1)S(1)}, bf16[4,6,512,128]{3,2,1,0:T(8,128)(2,1)}, u32[]{:S(2)}) copy-start(bf16[4,6,512,128]{3,2,1,0:T(8,128)(2,1)} %param.10) | copy-start | bytes 9437188
  7.2 47.2 %reduce-scatter.5.cloned.1.call-start = ((), (), s32[]{:S(2)}) async-start(), calls=%async_computation.4 | async-start | bytes 1310720 | tf_op jit(solution)/shard_map/reduce_scatter | solution.py:54
  7.2 8.2 %collective-permute-start = (bf16[4,128,128]{2,1,0:T(8,128)(2,1)}, bf16[4,128,128]{2,1,0:T(8,128)(2,1)S(1)}, u32[]{:S(2)}, u32[]{:S(2)}) collective-permute-start(bf16[4,128,128]{2,1,0:T(8,128)(2,1)} %param.13), channel_id=1, source_target_pairs={{0,4},{4,8},{8,12},{12,16},{16,20},{20,24},{24,28},{1,5},{5,9},{9,... | collective-permute-start | bytes 393224 | tf_op jit(solution)/shard_map/ppermute | solution.py:17
  12.4 7.2 %collective-permute-start.1 = (bf16[4,128,128]{2,1,0:T(8,128)(2,1)}, bf16[4,128,128]{2,1,0:T(8,128)(2,1)}, u32[]{:S(2)}, u32[]{:S(2)}) collective-permute-start(bf16[4,128,128]{2,1,0:T(8,128)(2,1)} %param.13), channel_id=1, source_target_pairs={{4,0},{8,4},{12,8},{16,12},{20,16},{24,20},{28,24},{5,1},{9,5},{13... | collective-permute-start | bytes 393224 | tf_op jit(solution)/shard_map/ppermute | solution.py:18
  15.4 0.7 copy-start.8
  24.5 2.4 copy-start.1
  24.5 2.4 copy-start.7
  26.9 27.5 %copy-start.9 = (f32[4,128]{1,0:T(4,128)S(1)}, f32[4,128]{1,0:T(4,128)}, u32[]{:S(2)}) copy-start(f32[4,128]{1,0:T(4,128)} %param.12) | copy-start | bytes 6148
  28.3 67.7 %reduce-scatter.7.cloned.1.call-start = ((), (), s32[]{:S(2)}) async-start(), calls=%async_computation.5 | async-start | bytes 1310720 | tf_op jit(solution)/shard_map/reduce_scatter | solution.py:54
  55.4 10.3 %copy-start.5 = (bf16[4,128,128]{1,2,0:T(8,128)(2,1)}, bf16[4,128,128]{1,2,0:T(8,128)(2,1)S(1)}, u32[]{:S(2)}) copy-start(bf16[4,128,128]{1,2,0:T(8,128)(2,1)S(1)} %subtract_convert_fusion.1) | copy-start | bytes 393220
  55.4 5.9 %collective-permute-start.2 = (bf16[4,128,128]{1,2,0:T(8,128)(2,1)S(1)}, bf16[4,128,128]{1,2,0:T(8,128)(2,1)S(1)}, u32[]{:S(2)}, u32[]{:S(2)}) collective-permute-start(bf16[4,128,128]{1,2,0:T(8,128)(2,1)S(1)} %subtract_convert_fusion.1), channel_id=1, source_target_pairs={{0,4},{4,8},{8,12},{12,16},{16,20},{20,24},{24,28},{1,5},{5,9},{9,... | collective-permute-start | bytes 393224 | tf_op jit(solution)/shard_map/ppermute | solution.py:17
  58.8 6.9 %collective-permute-start.3 = (bf16[4,128,128]{1,2,0:T(8,128)(2,1)S(1)}, bf16[4,128,128]{1,2,0:T(8,128)(2,1)S(1)}, u32[]{:S(2)}, u32[]{:S(2)}) collective-permute-start(bf16[4,128,128]{1,2,0:T(8,128)(2,1)S(1)} %subtract_convert_fusion.1), channel_id=1, source_target_pairs={{4,0},{8,4},{12,8},{16,12},{20,16},{24,20},{28,24},{5,1},{9,5},{13... | collective-permute-start | bytes 393224 | tf_op jit(solution)/shard_map/ppermute | solution.py:18
  67.3 2.4 copy-start.2
  67.3 2.4 copy-start.6
  69.6 1.4 copy-start.10
  69.6 1.5 copy-start.11
  69.7 1.6 copy-start.15
  71.0 68.7 %reduce-scatter.11.cloned.1.call-start = ((), (), s32[]{:S(2)}) async-start(), calls=%async_computation.7 | async-start | bytes 163840 | tf_op jit(solution)/shard_map/reduce_scatter | solution.py:93
  71.4 37.3 %copy-start.12 = (s32[4]{0:T(128)}, s32[4]{0:T(128)S(1)}, u32[]{:S(2)}) copy-start(s32[4]{0:T(128)S(1)} %select_reduce_fusion.2) | copy-start | bytes 52
  96.9 11.8 %copy-start.3 = (bf16[4,128,128]{1,2,0:T(8,128)(2,1)}, bf16[4,128,128]{1,2,0:T(8,128)(2,1)S(1)}, u32[]{:S(2)}) copy-start(bf16[4,128,128]{1,2,0:T(8,128)(2,1)S(1)} %subtract_convert_fusion) | copy-start | bytes 393220
  96.9 15.8 %copy-start.14 = (f32[4,6]{1,0:T(4,128)S(1)}, f32[4,6]{1,0:T(4,128)}, u32[]{:S(2)}) copy-start(f32[4,6]{1,0:T(4,128)} %copy.46) | copy-start | bytes 292
  96.9 11.8 %collective-permute-start.4 = (bf16[4,128,128]{1,2,0:T(8,128)(2,1)S(1)}, bf16[4,128,128]{1,2,0:T(8,128)(2,1)S(1)}, u32[]{:S(2)}, u32[]{:S(2)}) collective-permute-start(bf16[4,128,128]{1,2,0:T(8,128)(2,1)S(1)} %subtract_convert_fusion), channel_id=1, source_target_pairs={{0,4},{4,8},{8,12},{12,16},{16,20},{20,24},{24,28},{1,5},{5,9},{9,... | collective-permute-start | bytes 393224 | tf_op jit(solution)/shard_map/ppermute | solution.py:17
  100.5 8.3 %collective-permute-start.5 = (bf16[4,128,128]{1,2,0:T(8,128)(2,1)S(1)}, bf16[4,128,128]{1,2,0:T(8,128)(2,1)S(1)}, u32[]{:S(2)}, u32[]{:S(2)}) collective-permute-start(bf16[4,128,128]{1,2,0:T(8,128)(2,1)S(1)} %subtract_convert_fusion), channel_id=1, source_target_pairs={{4,0},{8,4},{12,8},{16,12},{20,16},{24,20},{28,24},{5,1},{9,5},{13... | collective-permute-start | bytes 393224 | tf_op jit(solution)/shard_map/ppermute | solution.py:18
  112.7 2.9 %copy-start.4 = (bf16[4,128,128]{1,2,0:T(8,128)(2,1)S(1)}, bf16[4,128,128]{1,2,0:T(8,128)(2,1)}, u32[]{:S(2)}) copy-start(bf16[4,128,128]{1,2,0:T(8,128)(2,1)} %copy-done.3) | copy-start | bytes 393220
  112.7 27.0 %copy-start.13 = (s32[4]{0:T(128)S(1)}, s32[4]{0:T(128)}, u32[]{:S(2)}) copy-start(s32[4]{0:T(128)} %copy-done.12) | copy-start | bytes 52
  118.0 43.6 %reduce-scatter.9.cloned.1.call-start = ((), (), s32[]{:S(2)}) async-start(), calls=%async_computation.6 | async-start | bytes 163840 | tf_op jit(solution)/shard_map/reduce_scatter | solution.py:90
  118.6 117.4 %all-reduce.2.cloned.1.call-start = ((), (), s32[]{:S(2)}) async-start(), calls=%async_computation.8 | async-start | bytes 262144 | tf_op jit(solution)/shard_map/psum | solution.py:116
Sparse Core Ops, SparseCore 0:
  28.4 25.9 reduce-scatter.4
  71.1 24.7 reduce-scatter.6
  118.1 21.4 reduce-scatter.10
  141.9 19.6 reduce-scatter.8
  165.4 70.5 all-reduce.1
where the time goes:
time: 245 us; the launch traced here: 244 us
  waiting for transfers between devices  142 us (58%)
  blocking collectives  38.1 us (16%)
  starting transfers between devices  16.1 us (7%)
  local copies, waits for them, and re-layouts  14.7 us (6%)
  matrix products  14.5 us (6%)
  between operations  14 us (6%)
  other arithmetic  4.53 us (2%)
    reduce_scatter x2, waiting for transfers between devices, body(): lax.psum_scatter(total_result.reshape(lax.axis_size('blk') * slab_rows, l...  48.6 us
    psum x1, waiting for transfers between devices, body(): last_level = lax.psum(level_terms, 'elem')  42.4 us
    all_gather x1, blocking collectives, body(): lax.all_gather(first_rows.astype(jnp.bfloat16), 'elem', axis=0, tiled=True)  31.1 us
    reduce_scatter x1, waiting for transfers between devices, body(): lax.psum_scatter(second_level_sum.astype(jnp.bfloat16), 'blk', scatter_di...  20.2 us
    reduce_scatter x1, waiting for transfers between devices, body(): lax.psum_scatter(first_sum.astype(jnp.bfloat16), 'blk', scatter_dimension...  20.2 us
    ppermute x3, starting transfers between devices, extended(): before = lax.ppermute(last, axis, up)  12 us
    gather x5, local copies, waits for them, and re-layouts, nearby_slabs(): return jnp.take(padded, offsets, axis=0)  9.3 us
    ppermute x3, waiting for transfers between devices, extended(): after = lax.ppermute(initial, axis, down)  7.77 us
  transfers between devices with their start and end apart: 11, of which 9 were waited for; matrix products, arithmetic and copies ran while one was open for 3% of the time, Pallas kernels for 0%

commit v1 on v0

v1 whole, which is shorter than its diff:
```python
import functools

import jax
import jax.numpy as jnp
from jax import lax
from jax.experimental import pallas as pl
from jax.experimental.pallas import tpu as pltpu
from jax.sharding import PartitionSpec as P

SWEEPS = 2
NG = 8
VMEM = pl.BlockSpec(memory_space=pltpu.VMEM)
SMEM = pl.BlockSpec(memory_space=pltpu.SMEM)


def call(kernel, ins, outs, scratch, flops, *args):
    return pl.pallas_call(
        kernel,
        in_specs=ins,
        out_specs=[VMEM] * len(outs),
        out_shape=outs,
        scratch_shapes=scratch,
        compiler_params=pltpu.CompilerParams(vmem_limit_bytes=24 << 20),
        cost_estimate=pl.CostEstimate(flops=flops, bytes_accessed=4 << 20, transcendentals=0),
    )(*args)


def flip(x, axis, bit):
    size = lax.axis_size(axis)
    return lax.ppermute(x, axis, [(i, i ^ bit) for i in range(size) if i ^ bit < size])


def beside(x):
    size = lax.axis_size("elem")
    across = [(i, i + 1) for i in range(1, size - 1, 2)]
    return flip(x, "elem", 1), lax.ppermute(x, "elem", across + [(j, i) for i, j in across])


def scatter_sum(keep, send):
    bit = 1
    while True:
        total = keep + flip(send, "blk", bit)
        if total.shape[0] == 1:
            return total[0]
        keep, send = total[0::2], total[1::2].astype(jnp.bfloat16)
        bit *= 2


def gathered(x):
    parts = {0: x}
    bit = lax.axis_size("blk") // 2
    while bit:
        order = sorted(parts)
        other = flip(jnp.stack([parts[r] for r in order]), "blk", bit)
        for at, r in enumerate(order):
            parts[r + bit] = other[at]
        bit //= 2
    return jnp.stack([parts[r] for r in range(len(parts))])


def slot(pos_ref, element, count):
    position = pos_ref[0]
    offset = element - position * count
    even = position % 2 == 0
    below = jnp.where(even, 3 * count, 2 * count)
    above = jnp.where(even, 0, count)
    return offset + jnp.where(offset < 0, below, jnp.where(offset < count, 0, above))


def fill(slabs, own, pair, across):
    count = own.shape[0]
    slabs[0:count] = own[...]
    slabs[count : 2 * count] = pair[...]
    slabs[2 * count : 3 * count] = across[...]


def split_rows(pos_ref, value, part_ref, keep_ref, send_ref, at):
    chunks, rows = part_ref.shape[0], part_ref.shape[1]
    for j in range(chunks):
        part_ref[j] = value[j * rows : (j + 1) * rows]
    me = pos_ref[1]
    for r in range(chunks):
        chunk = part_ref[me ^ r]
        if r % 2 == 0:
            keep_ref[r // 2, at] = chunk
        else:
            send_ref[r // 2, at] = chunk.astype(send_ref.dtype)


def sweep_kernel(pos, nbrs, diag, blocks, own, pair, across, keep, send, slabs, part):
    count, faces = blocks.shape[0], blocks.shape[1]
    fill(slabs, own, pair, across)
    for i in range(count):
        left = [diag[i]] + [blocks[i, k] for k in range(faces)]
        right = [own[i]] + [slabs[slot(pos, nbrs[i, k], count)] for k in range(faces)]
        y = jnp.dot(
            jnp.concatenate(left, axis=1),
            jnp.concatenate(right, axis=0),
            preferred_element_type=jnp.float32,
        )
        split_rows(pos, y, part, keep, send, i)


def couple_kernel(
    pos, nbrs, agg, group, diag, blocks, every, pair, across, keep, send, slabs, part
):
    count, faces = blocks.shape[0], blocks.shape[1]
    width = pair.shape[2]
    fill(slabs, every.at[0], pair, across)
    first = pos[0] * count
    for i in range(count):
        rows = [every[pos[1] ^ j, i] for j in range(every.shape[0])]
        left = [diag[i]] + [blocks[i, k] for k in range(faces)]
        w = lax.dot_general(
            jnp.concatenate(rows, axis=0),
            jnp.concatenate(left, axis=1),
            (((0,), (0,)), ((), ())),
            preferred_element_type=jnp.float32,
        ).astype(jnp.bfloat16)
        own_agg = agg[first + i]
        own_group = group[own_agg]
        right = [jnp.concatenate([slabs[i], slabs[i]], axis=1)]
        for k in range(faces):
            near = nbrs[i, k]
            near_agg = agg[near]
            slab = slabs[slot(pos, near, count)]
            none = jnp.zeros_like(slab)
            right.append(
                jnp.concatenate(
                    [
                        jnp.where(near_agg == own_agg, slab, none),
                        jnp.where(group[near_agg] == own_group, slab, none),
                    ],
                    axis=1,
                )
            )
        t = jnp.dot(w, jnp.concatenate(right, axis=0), preferred_element_type=jnp.float32)
        split_rows(pos, t[:, :width], part, keep, send, i)
        split_rows(pos, t[:, width:], part, keep, send, count + i)


def pack_kernel(pos, agg, total, out, sums):
    count = total.shape[0] // 2
    owned = out.shape[1] - count
    sums[...] = jnp.zeros_like(sums)
    for i in range(count):
        at = agg[pos[0] * count + i]
        sums[at] = sums[at] + total[i]

    def one(dest, carry):
        for j in range(owned):
            out[dest, j] = sums[dest * owned + j].astype(out.dtype)
        out[dest, owned:] = total[count:].astype(out.dtype)
        return carry

    lax.fori_loop(0, out.shape[0], one, 0)


def finish_kernel(agg, group, parts, coarse, last, *, count):
    owned = coarse.shape[0]
    coarse[...] = jnp.zeros_like(coarse)
    last[...] = jnp.zeros_like(last)

    def one(source, carry):
        coarse[...] = coarse[...] + parts[source, :owned].astype(jnp.float32)
        for i in range(count):
            at = group[agg[source * count + i]]
            last[at] = last[at] + parts[source, owned + i].astype(jnp.float32)
        return carry

    lax.fori_loop(0, parts.shape[0], one, 0)


def body(diag, blocks, neighbours, damping, bases, agglomerate, group):
    count, rows, width = bases.shape
    faces = neighbours.shape[1]
    ways = lax.axis_size("blk")
    size = lax.axis_size("elem")
    pos = jnp.stack([lax.axis_index("elem"), lax.axis_index("blk")]).astype(jnp.int32)
    f32, bf16 = jnp.float32, jnp.bfloat16
    slabs = pltpu.VMEM((3 * count, rows, width), bf16)
    shape = jax.ShapeDtypeStruct
    flops = 2 * count * (faces + 1) * ways * rows * rows * width

    x = bases
    pair, across = beside(x)
    for _ in range(SWEEPS):
        keep, send = call(
            sweep_kernel,
            [SMEM, SMEM] + [VMEM] * 5,
            [
                shape((ways // 2, count, rows, width), f32),
                shape((ways // 2, count, rows, width), bf16),
            ],
            [slabs, pltpu.VMEM((ways, rows, width), f32)],
            flops,
            *(pos, neighbours, diag, blocks, x, pair, across),
        )
        total = scatter_sum(keep, send)
        x = (x.astype(f32) - damping[:, :, None] * total).astype(bf16)
        pair, across = beside(x)

    every = gathered(x)
    part = width // ways
    keep, send = call(
        couple_kernel,
        [SMEM] * 4 + [VMEM] * 5,
        [
            shape((ways // 2, 2 * count, part, width), f32),
            shape((ways // 2, 2 * count, part, width), bf16),
        ],
        [slabs, pltpu.VMEM((ways, part, width), f32)],
        flops,
        *(pos, neighbours, agglomerate, group, diag, blocks, every, pair, across),
    )
    total = scatter_sum(keep, send)

    owned = group.shape[0] // size
    (parts,) = call(
        pack_kernel,
        [SMEM, SMEM, VMEM],
        [shape((size, owned + count, part, width), bf16)],
        [pltpu.VMEM((group.shape[0], part, width), f32)],
        1 << 20,
        *(pos, agglomerate, total),
    )
    parts = lax.all_to_all(parts, "elem", 0, 0, tiled=True)
    coarse, last = call(
        functools.partial(finish_kernel, count=count),
        [SMEM, SMEM, VMEM],
        [shape((owned, part, width), f32), shape((NG, part, width), f32)],
        [],
        1 << 20,
        *(agglomerate, group, parts),
    )
    return x, coarse, last


def solution(mesh):
    return jax.shard_map(
        body,
        mesh=mesh,
        in_specs=(
            P("elem", None, "blk"),
            P("elem", None, None, "blk"),
            P("elem", None),
            P("elem", "blk"),
            P("elem", "blk", None),
            P(),
            P(),
        ),
        out_specs=(P("elem", "blk", None), P("elem", "blk", None), P(None, "blk", None)),
        check_vma=False,
    )
```

time: 245 us -> 86.7 us (0.35)
  waiting for transfers between devices: 142 us -> 29.1 us
  blocking collectives: 38.1 us -> 17.2 us
  matrix products: 14.5 us -> 0 us
  between operations: 14 us -> 0.84 us
  starting transfers between devices: 16.1 us -> 26.8 us
  local copies, waits for them, and re-layouts: 14.7 us -> 4.61 us
  Pallas kernels: 0 us -> 7.28 us
  other arithmetic: 4.53 us -> 0.61 us
    reduce_scatter x4 -> x0, waiting for transfers between devices: 89.1 us -> none  [the longest x2 48.6 us: body(): lax.psum_scatter(total_result.reshape(lax.axis_size('blk') * slab_rows, l...]
    psum x1 -> x0, waiting for transfers between devices: 42.4 us -> none  [body(): last_level = lax.psum(level_terms, 'elem')]
    all_gather x2 -> x0, blocking collectives: 38.1 us -> none  [the longest x1 31.1 us: body(): lax.all_gather(first_rows.astype(jnp.bfloat16), 'elem', axis=0, tiled=True)]
    ppermute x6 -> x14, waiting for transfers between devices: 10 us -> 29.1 us  [the longest x11 29.1 us: flip(): lax.ppermute(x, axis, [(i, i ^ bit) for i in range(size) if i ^ bit < size])]
    all_to_all x0 -> x1, blocking collectives: none -> 17.2 us  [body(): parts = lax.all_to_all(parts, 'elem', 0, 0, tiled=True)]
    dot_general x8 -> x0, matrix products: 14.5 us -> none  [the longest x2 4.69 us: body(): jnp.einsum('psgw,pswj->gpj', neighbour_block_list, nearby_elements, prefe...]
    ppermute x6 -> x14, starting transfers between devices: 15.9 us -> 26.8 us  [the longest x11 24.8 us: flip(): lax.ppermute(x, axis, [(i, i ^ bit) for i in range(size) if i ^ bit < size])]
    gather x5 -> x0, local copies, waits for them, and re-layouts: 9.3 us -> none  [nearby_slabs(): return jnp.take(padded, offsets, axis=0)]
  transfers between devices with their start and end apart: 11 -> 14, of which waited for: 9 -> 10; matrix products, arithmetic and copies ran while one was open for 3% -> 0% of each run, Pallas kernels for 0% -> 0%
where the time goes in v1:
time: 86.7 us; the launch traced here: 86.4 us
  waiting for transfers between devices  29.1 us (34%)
  starting transfers between devices  26.8 us (31%)
  blocking collectives  17.2 us (20%)
  Pallas kernels  7.28 us (8%)
  local copies, waits for them, and re-layouts  4.61 us (5%)
    ppermute x11, waiting for transfers between devices, flip(): lax.ppermute(x, axis, [(i, i ^ bit) for i in range(size) if i ^ bit < size])  29.1 us
    ppermute x11, starting transfers between devices, flip(): lax.ppermute(x, axis, [(i, i ^ bit) for i in range(size) if i ^ bit < size])  24.8 us
    all_to_all x1, blocking collectives, body(): parts = lax.all_to_all(parts, 'elem', 0, 0, tiled=True)  17.2 us
    pallas_call x5, Pallas kernels, call(): pl.pallas_call(kernel, in_specs=ins, out_specs=[VMEM] * len(outs), out_sh...  7.28 us
    unnamed x16, local copies, waits for them, and re-layouts  4.54 us
    ppermute x3, starting transfers between devices, beside(): lax.ppermute(x, 'elem', across + [(j, i) for i, j in across])  1.99 us
  transfers between devices with their start and end apart: 14, of which 10 were waited for; matrix products, arithmetic and copies ran while one was open for 0% of the time, Pallas kernels for 0%

profile of v1, /device:TPU:0, one launch (start us, length us, event | category | flops | bytes accessed | tf_op | source)
XLA Modules:
  0.0 86.4 jit_solution(5512514733954040617)
XLA Ops:
  0.6 0.0 copy-start.7
  0.6 3.0 %collective-permute-start = (bf16[4,128,128]{2,1,0:T(8,128)(2,1)}, bf16[4,128,128]{2,1,0:T(8,128)(2,1)S(1)}, u32[]{:S(2)}, u32[]{:S(2)}) collective-permute-start(bf16[4,128,128]{2,1,0:T(8,128)(2,1)} %own.1), channel_id=1, source_target_pairs={{0,4},{4,0},{8,12},{12,8},{16,20},{20,16},{24,28},{28,24},{1,5},{5... | collective-permute-start | bytes 393224 | tf_op jit(solution)/shard_map/ppermute | solution.py:30
  3.7 0.7 collective-permute-start.1
  4.3 0.1 pad_add_fusion.pos
  4.4 3.0 %collective-permute-done.pair = bf16[4,128,128]{2,1,0:T(8,128)(2,1)S(1)} collective-permute-done((bf16[4,128,128]{2,1,0:T(8,128)(2,1)}, bf16[4,128,128]{2,1,0:T(8,128)(2,1)S(1)}, u32[]{:S(2)}, u32[]{:S(2)}) %collective-permute-start) | collective-permute-done | bytes 131104 | tf_op jit(solution)/shard_map/ppermute | solution.py:30
  7.4 0.0 collective-permute-done.1.across
  7.4 1.9 %copy-done = bf16[4,6,512,128]{3,2,1,0:T(8,128)(2,1)S(1)} copy-done((bf16[4,6,512,128]{3,2,1,0:T(8,128)(2,1)S(1)}, bf16[4,6,512,128]{3,2,1,0:T(8,128)(2,1)}, u32[]{:S(2)}) %copy-start) | copy-done | bytes 3145752
  9.3 1.0 %copy-done.1 = bf16[4,512,128]{2,1,0:T(8,128)(2,1)S(1)} copy-done((bf16[4,512,128]{2,1,0:T(8,128)(2,1)S(1)}, bf16[4,512,128]{2,1,0:T(8,128)(2,1)}, u32[]{:S(2)}) %copy-start.1) | copy-done | bytes 524312
  10.3 0.9 %copy-done.2 = bf16[4,128,128]{2,1,0:T(8,128)(2,1)S(1)} copy-done((bf16[4,128,128]{2,1,0:T(8,128)(2,1)S(1)}, bf16[4,128,128]{2,1,0:T(8,128)(2,1)}, u32[]{:S(2)}) %copy-start.2) | copy-done | bytes 131096
  11.2 0.7 copy-done.3
  11.9 1.7 %shard_map.94 = (f32[2,4,128,128]{3,2,1,0:T(8,128)S(1)}, bf16[2,4,128,128]{3,2,1,0:T(8,128)(2,1)S(1)}) custom-call(s32[2]{0:T(128)S(1)} %pad_add_fusion.pos, s32[4,6]{1,0:T(4,128)S(1)} %copy-done.3, bf16[4,512,128]{2,1,0:T(8,128)(2,1)S(1)} %copy-done.1, bf16[4,6,512,128]{3,2,1,0:T(8,128)(2,1)S(1)} %copy-done, bf16[4,128,128]{2,1,0:T(8,128)(2,1)S(1)} %copy-done.2, ...), custom_call_target="tpu_custom_call" | custom-call | flops 469762048 | bytes 4194304 | tf_op jit(solution)/shard_map/pallas_call | solution.py:17
  13.6 0.1 collective-permute-start.2
  13.7 1.5 %collective-permute-done.2 = bf16[2,4,128,128]{3,2,1,0:T(8,128)(2,1)S(1)} collective-permute-done((bf16[2,4,128,128]{3,2,1,0:T(8,128)(2,1)S(1)}, bf16[2,4,128,128]{3,2,1,0:T(8,128)(2,1)S(1)}, u32[]{:S(2)}, u32[]{:S(2)}) %collective-permute-start.2) | collective-permute-done | bytes 262176 | tf_op jit(solution)/shard_map/ppermute | solution.py:30
  15.3 1.8 %collective-permute-start.3 = (bf16[1,4,128,128]{3,2,1,0:T(8,128)(2,1)S(1)}, bf16[1,4,128,128]{3,2,1,0:T(8,128)(2,1)S(1)}, u32[]{:S(2)}, u32[]{:S(2)}) collective-permute-start(bf16[1,4,128,128]{3,2,1,0:T(8,128)(2,1)S(1)} %slice.74), channel_id=1, source_target_pairs={{0,2},{1,3},{2,0},{3,1},{4,6},{5,7},{6,4},{7,5},{8,10},{9,11},{10,... | collective-permute-start | bytes 393224 | tf_op jit(solution)/shard_map/ppermute | solution.py:30
  17.2 3.8 %collective-permute-done.3 = bf16[1,4,128,128]{3,2,1,0:T(8,128)(2,1)S(1)} collective-permute-done((bf16[1,4,128,128]{3,2,1,0:T(8,128)(2,1)S(1)}, bf16[1,4,128,128]{3,2,1,0:T(8,128)(2,1)S(1)}, u32[]{:S(2)}, u32[]{:S(2)}) %collective-permute-start.3) | collective-permute-done | bytes 131104 | tf_op jit(solution)/shard_map/ppermute | solution.py:30
  21.0 0.1 fusion.7.own
  21.1 0.7 collective-permute-start.5
  21.8 8.6 %collective-permute-start.4 = (bf16[4,128,128]{2,1,0:T(8,128)(2,1)S(1)}, bf16[4,128,128]{2,1,0:T(8,128)(2,1)S(1)}, u32[]{:S(2)}, u32[]{:S(2)}) collective-permute-start(bf16[4,128,128]{2,1,0:T(8,128)(2,1)S(1)} %fusion.7.own), channel_id=1, source_target_pairs={{0,4},{4,0},{8,12},{12,8},{16,20},{20,16},{24,28},{28,24},{1,5},{5... | collective-permute-start | bytes 393224 | tf_op jit(solution)/shard_map/ppermute | solution.py:30
  30.3 0.0 collective-permute-done.5.across
  30.3 3.3 %collective-permute-done.4.pair = bf16[4,128,128]{2,1,0:T(8,128)(2,1)S(1)} collective-permute-done((bf16[4,128,128]{2,1,0:T(8,128)(2,1)S(1)}, bf16[4,128,128]{2,1,0:T(8,128)(2,1)S(1)}, u32[]{:S(2)}, u32[]{:S(2)}) %collective-permute-start.4) | collective-permute-done | bytes 131104 | tf_op jit(solution)/shard_map/ppermute | solution.py:30
  33.7 1.7 %shard_map.95 = (f32[2,4,128,128]{3,2,1,0:T(8,128)S(1)}, bf16[2,4,128,128]{3,2,1,0:T(8,128)(2,1)S(1)}) custom-call(s32[2]{0:T(128)S(1)} %pad_add_fusion.pos, s32[4,6]{1,0:T(4,128)S(1)} %copy-done.3, bf16[4,512,128]{2,1,0:T(8,128)(2,1)S(1)} %copy-done.1, bf16[4,6,512,128]{3,2,1,0:T(8,128)(2,1)S(1)} %copy-done, bf16[4,128,128]{2,1,0:T(8,128)(2,1)S(1)} %fusion.7.own, ...), custom_call_target="tpu_custom_call" | custom-call | flops 469762048 | bytes 4194304 | tf_op jit(solution)/shard_map/pallas_call | solution.py:17
  35.4 0.0 copy-start.4
  35.4 0.0 copy-start.5
  35.4 0.1 collective-permute-start.6
  35.5 1.5 %collective-permute-done.6 = bf16[2,4,128,128]{3,2,1,0:T(8,128)(2,1)S(1)} collective-permute-done((bf16[2,4,128,128]{3,2,1,0:T(8,128)(2,1)S(1)}, bf16[2,4,128,128]{3,2,1,0:T(8,128)(2,1)S(1)}, u32[]{:S(2)}, u32[]{:S(2)}) %collective-permute-start.6) | collective-permute-done | bytes 262176 | tf_op jit(solution)/shard_map/ppermute | solution.py:30
  37.0 0.1 convert_add_fusion
  37.1 1.6 %collective-permute-start.7 = (bf16[1,4,128,128]{3,2,1,0:T(8,128)(2,1)S(1)}, bf16[1,4,128,128]{3,2,1,0:T(8,128)(2,1)S(1)}, u32[]{:S(2)}, u32[]{:S(2)}) collective-permute-start(bf16[1,4,128,128]{3,2,1,0:T(8,128)(2,1)S(1)} %slice.73), channel_id=1, source_target_pairs={{0,2},{1,3},{2,0},{3,1},{4,6},{5,7},{6,4},{7,5},{8,10},{9,11},{10,... | collective-permute-start | bytes 393224 | tf_op jit(solution)/shard_map/ppermute | solution.py:30
  38.7 4.0 %collective-permute-done.7 = bf16[1,4,128,128]{3,2,1,0:T(8,128)(2,1)S(1)} collective-permute-done((bf16[1,4,128,128]{3,2,1,0:T(8,128)(2,1)S(1)}, bf16[1,4,128,128]{3,2,1,0:T(8,128)(2,1)S(1)}, u32[]{:S(2)}, u32[]{:S(2)}) %collective-permute-start.7) | collective-permute-done | bytes 131104 | tf_op jit(solution)/shard_map/ppermute | solution.py:30
  42.7 0.1 fusion.3
  42.9 0.0 copy-start.6
  42.9 1.6 %collective-permute-start.8 = (bf16[1,4,128,128]{3,2,1,0:T(8,128)(2,1)S(1)}, bf16[1,4,128,128]{3,2,1,0:T(8,128)(2,1)S(1)}, u32[]{:S(2)}, u32[]{:S(2)}) collective-permute-start(bf16[1,4,128,128]{3,2,1,0:T(8,128)(2,1)S(1)} %bitcast.21), channel_id=1, source_target_pairs={{0,2},{1,3},{2,0},{3,1},{4,6},{5,7},{6,4},{7,5},{8,10},{9,11},{10,... | collective-permute-start | bytes 393224 | tf_op jit(solution)/shard_map/ppermute | solution.py:30
  44.5 3.4 %collective-permute-done.8 = bf16[1,4,128,128]{3,2,1,0:T(8,128)(2,1)S(1)} collective-permute-done((bf16[1,4,128,128]{3,2,1,0:T(8,128)(2,1)S(1)}, bf16[1,4,128,128]{3,2,1,0:T(8,128)(2,1)S(1)}, u32[]{:S(2)}, u32[]{:S(2)}) %collective-permute-start.8) | collective-permute-done | bytes 131104 | tf_op jit(solution)/shard_map/ppermute | solution.py:30
  47.9 0.1 collective-permute-start.9
  48.0 0.7 collective-permute-start.11
  48.7 6.3 %collective-permute-start.10 = (bf16[4,128,128]{2,1,0:T(8,128)(2,1)S(1)}, bf16[4,128,128]{2,1,0:T(8,128)(2,1)S(1)}, u32[]{:S(2)}, u32[]{:S(2)}) collective-permute-start(bf16[4,128,128]{2,1,0:T(8,128)(2,1)S(1)} %fusion.3), channel_id=1, source_target_pairs={{0,4},{4,0},{8,12},{12,8},{16,20},{20,16},{24,28},{28,24},{1,5},{5... | collective-permute-start | bytes 393224 | tf_op jit(solution)/shard_map/ppermute | solution.py:30
  55.0 0.0 collective-permute-done.9
  55.0 0.1 pad_maximum_fusion.every
  55.1 0.0 collective-permute-done.11.across
  55.1 4.4 %collective-permute-done.10.pair = bf16[4,128,128]{2,1,0:T(8,128)(2,1)S(1)} collective-permute-done((bf16[4,128,128]{2,1,0:T(8,128)(2,1)S(1)}, bf16[4,128,128]{2,1,0:T(8,128)(2,1)S(1)}, u32[]{:S(2)}, u32[]{:S(2)}) %collective-permute-start.10) | collective-permute-done | bytes 131104 | tf_op jit(solution)/shard_map/ppermute | solution.py:30
  59.5 0.0 copy-done.5
  59.5 1.8 %shard_map.96 = (f32[2,8,32,128]{3,2,1,0:T(8,128)S(1)}, bf16[2,8,32,128]{3,2,1,0:T(8,128)(2,1)S(1)}) custom-call(s32[2]{0:T(128)S(1)} %pad_add_fusion.pos, s32[4,6]{1,0:T(4,128)S(1)} %copy-done.3, s32[32]{0:T(128)S(1)} %copy-done.4, s32[16]{0:T(128)S(1)} %copy-done.5, bf16[4,512,128]{2,1,0:T(8,128)(2,1)S(1)} %copy-done.1, ...), custom_call_target="tpu_custom_call" | custom-call | flops 469762048 | bytes 4194304 | tf_op jit(solution)/shard_map/pallas_call | solution.py:17
  61.3 0.1 collective-permute-start.12
  61.5 1.3 %collective-permute-done.12 = bf16[2,8,32,128]{3,2,1,0:T(8,128)(2,1)S(1)} collective-permute-done((bf16[2,8,32,128]{3,2,1,0:T(8,128)(2,1)S(1)}, bf16[2,8,32,128]{3,2,1,0:T(8,128)(2,1)S(1)}, u32[]{:S(2)}, u32[]{:S(2)}) %collective-permute-start.12) | collective-permute-done | bytes 131104 | tf_op jit(solution)/shard_map/ppermute | solution.py:30
  62.8 1.6 %collective-permute-start.13 = (bf16[1,8,32,128]{3,2,1,0:T(8,128)(2,1)S(1)}, bf16[1,8,32,128]{3,2,1,0:T(8,128)(2,1)S(1)}, u32[]{:S(2)}, u32[]{:S(2)}) collective-permute-start(bf16[1,8,32,128]{3,2,1,0:T(8,128)(2,1)S(1)} %slice.75), channel_id=1, source_target_pairs={{0,2},{1,3},{2,0},{3,1},{4,6},{5,7},{6,4},{7,5},{8,10},{9,11},{10,... | collective-permute-start | bytes 196616 | tf_op jit(solution)/shard_map/ppermute | solution.py:30
  64.4 2.7 %collective-permute-done.13 = bf16[1,8,32,128]{3,2,1,0:T(8,128)(2,1)S(1)} collective-permute-done((bf16[1,8,32,128]{3,2,1,0:T(8,128)(2,1)S(1)}, bf16[1,8,32,128]{3,2,1,0:T(8,128)(2,1)S(1)}, u32[]{:S(2)}, u32[]{:S(2)}) %collective-permute-start.13) | collective-permute-done | bytes 65568 | tf_op jit(solution)/shard_map/ppermute | solution.py:30
  67.2 0.6 shard_map.97
  67.8 17.2 %all_to_all.5.parts = bf16[8,6,32,128]{3,2,1,0:T(8,128)(2,1)S(1)} all-to-all(bf16[8,6,32,128]{3,2,1,0:T(8,128)(2,1)S(1)} %shard_map.97), channel_id=1, replica_groups=mesh['elem'=8,'blk'=4] {'elem'}, dimensions={0} | all-to-all | bytes 786432 | tf_op jit(solution)/shard_map/all_to_all | solution.py:227
  85.0 1.4 %shard_map.98 = (f32[2,32,128]{2,1,0:T(8,128)}, f32[8,32,128]{2,1,0:T(8,128)}) custom-call(s32[32]{0:T(128)S(1)} %copy-done.4, s32[16]{0:T(128)S(1)} %copy-done.5, bf16[8,6,32,128]{3,2,1,0:T(8,128)(2,1)S(1)} %all_to_all.5.parts), custom_call_target="tpu_custom_call" | custom-call | flops 1048576 | bytes 4194304 | tf_op jit(solution)/shard_map/pallas_call | solution.py:17
  (15 shorter events, 0.2 us)
Async XLA Ops:
  0.6 20.3 %copy-start.7 = (f32[4,128]{1,0:T(4,128)S(1)}, f32[4,128]{1,0:T(4,128)}, u32[]{:S(2)}) copy-start(f32[4,128]{1,0:T(4,128)} %param.10) | copy-start | bytes 6148
  0.6 6.7 %collective-permute-start = (bf16[4,128,128]{2,1,0:T(8,128)(2,1)}, bf16[4,128,128]{2,1,0:T(8,128)(2,1)S(1)}, u32[]{:S(2)}, u32[]{:S(2)}) collective-permute-start(bf16[4,128,128]{2,1,0:T(8,128)(2,1)} %own.1), channel_id=1, source_target_pairs={{0,4},{4,0},{8,12},{12,8},{16,20},{20,16},{24,28},{28,24},{1,5},{5... | collective-permute-start | bytes 393224 | tf_op jit(solution)/shard_map/ppermute | solution.py:30
  3.7 3.7 %collective-permute-start.1 = (bf16[4,128,128]{2,1,0:T(8,128)(2,1)}, bf16[4,128,128]{2,1,0:T(8,128)(2,1)S(1)}, u32[]{:S(2)}, u32[]{:S(2)}) collective-permute-start(bf16[4,128,128]{2,1,0:T(8,128)(2,1)} %own.1), channel_id=1, source_target_pairs={{4,8},{12,16},{20,24},{8,4},{16,12},{24,20},{5,9},{13,17},{21,25},... | collective-permute-start | bytes 393224 | tf_op jit(solution)/shard_map/ppermute | solution.py:36
  7.4 1.9 %copy-start = (bf16[4,6,512,128]{3,2,1,0:T(8,128)(2,1)S(1)}, bf16[4,6,512,128]{3,2,1,0:T(8,128)(2,1)}, u32[]{:S(2)}) copy-start(bf16[4,6,512,128]{3,2,1,0:T(8,128)(2,1)} %blocks.5) | copy-start | bytes 9437188
  9.3 1.0 %copy-start.1 = (bf16[4,512,128]{2,1,0:T(8,128)(2,1)S(1)}, bf16[4,512,128]{2,1,0:T(8,128)(2,1)}, u32[]{:S(2)}) copy-start(bf16[4,512,128]{2,1,0:T(8,128)(2,1)} %diag.5) | copy-start | bytes 1572868
  10.3 0.9 %copy-start.2 = (bf16[4,128,128]{2,1,0:T(8,128)(2,1)S(1)}, bf16[4,128,128]{2,1,0:T(8,128)(2,1)}, u32[]{:S(2)}) copy-start(bf16[4,128,128]{2,1,0:T(8,128)(2,1)} %own.1) | copy-start | bytes 393220
  11.2 0.7 copy-start.3
  13.6 1.6 %collective-permute-start.2 = (bf16[2,4,128,128]{3,2,1,0:T(8,128)(2,1)S(1)}, bf16[2,4,128,128]{3,2,1,0:T(8,128)(2,1)S(1)}, u32[]{:S(2)}, u32[]{:S(2)}) collective-permute-start(bf16[2,4,128,128]{3,2,1,0:T(8,128)(2,1)S(1)} %get-tuple-element.12), channel_id=1, source_target_pairs={{0,1},{1,0},{2,3},{3,2},{4,5},{5,4},{6,7},{7,6},{8,9},{9,8},{10,11... | collective-permute-start | bytes 786440 | tf_op jit(solution)/shard_map/ppermute | solution.py:30
  15.3 5.6 %collective-permute-start.3 = (bf16[1,4,128,128]{3,2,1,0:T(8,128)(2,1)S(1)}, bf16[1,4,128,128]{3,2,1,0:T(8,128)(2,1)S(1)}, u32[]{:S(2)}, u32[]{:S(2)}) collective-permute-start(bf16[1,4,128,128]{3,2,1,0:T(8,128)(2,1)S(1)} %slice.74), channel_id=1, source_target_pairs={{0,2},{1,3},{2,0},{3,1},{4,6},{5,7},{6,4},{7,5},{8,10},{9,11},{10,... | collective-permute-start | bytes 393224 | tf_op jit(solution)/shard_map/ppermute | solution.py:30
  21.1 9.2 %collective-permute-start.5 = (bf16[4,128,128]{2,1,0:T(8,128)(2,1)S(1)}, bf16[4,128,128]{2,1,0:T(8,128)(2,1)S(1)}, u32[]{:S(2)}, u32[]{:S(2)}) collective-permute-start(bf16[4,128,128]{2,1,0:T(8,128)(2,1)S(1)} %fusion.7.own), channel_id=1, source_target_pairs={{4,8},{12,16},{20,24},{8,4},{16,12},{24,20},{5,9},{13,17},{21,25},... | collective-permute-start | bytes 393224 | tf_op jit(solution)/shard_map/ppermute | solution.py:36
  21.8 11.9 %collective-permute-start.4 = (bf16[4,128,128]{2,1,0:T(8,128)(2,1)S(1)}, bf16[4,128,128]{2,1,0:T(8,128)(2,1)S(1)}, u32[]{:S(2)}, u32[]{:S(2)}) collective-permute-start(bf16[4,128,128]{2,1,0:T(8,128)(2,1)S(1)} %fusion.7.own), channel_id=1, source_target_pairs={{0,4},{4,0},{8,12},{12,8},{16,20},{20,16},{24,28},{28,24},{1,5},{5... | collective-permute-start | bytes 393224 | tf_op jit(solution)/shard_map/ppermute | solution.py:30
  35.4 24.1 %copy-start.4 = (s32[32]{0:T(128)S(1)}, s32[32]{0:T(128)}, u32[]{:S(2)}) copy-start(s32[32]{0:T(128)} %agg.5) | copy-start | bytes 388
  35.4 24.1 %copy-start.5 = (s32[16]{0:T(128)S(1)}, s32[16]{0:T(128)}, u32[]{:S(2)}) copy-start(s32[16]{0:T(128)} %group.3) | copy-start | bytes 196
  35.4 1.6 %collective-permute-start.6 = (bf16[2,4,128,128]{3,2,1,0:T(8,128)(2,1)S(1)}, bf16[2,4,128,128]{3,2,1,0:T(8,128)(2,1)S(1)}, u32[]{:S(2)}, u32[]{:S(2)}) collective-permute-start(bf16[2,4,128,128]{3,2,1,0:T(8,128)(2,1)S(1)} %get-tuple-element.14), channel_id=1, source_target_pairs={{0,1},{1,0},{2,3},{3,2},{4,5},{5,4},{6,7},{7,6},{8,9},{9,8},{10,11... | collective-permute-start | bytes 786440 | tf_op jit(solution)/shard_map/ppermute | solution.py:30
  37.1 5.6 %collective-permute-start.7 = (bf16[1,4,128,128]{3,2,1,0:T(8,128)(2,1)S(1)}, bf16[1,4,128,128]{3,2,1,0:T(8,128)(2,1)S(1)}, u32[]{:S(2)}, u32[]{:S(2)}) collective-permute-start(bf16[1,4,128,128]{3,2,1,0:T(8,128)(2,1)S(1)} %slice.73), channel_id=1, source_target_pairs={{0,2},{1,3},{2,0},{3,1},{4,6},{5,7},{6,4},{7,5},{8,10},{9,11},{10,... | collective-permute-start | bytes 393224 | tf_op jit(solution)/shard_map/ppermute | solution.py:30
  42.9 18.5 %copy-start.6 = (bf16[4,128,128]{2,1,0:T(8,128)(2,1)}, bf16[4,128,128]{2,1,0:T(8,128)(2,1)S(1)}, u32[]{:S(2)}) copy-start(bf16[4,128,128]{2,1,0:T(8,128)(2,1)S(1)} %fusion.3) | copy-start | bytes 393220
  42.9 5.0 %collective-permute-start.8 = (bf16[1,4,128,128]{3,2,1,0:T(8,128)(2,1)S(1)}, bf16[1,4,128,128]{3,2,1,0:T(8,128)(2,1)S(1)}, u32[]{:S(2)}, u32[]{:S(2)}) collective-permute-start(bf16[1,4,128,128]{3,2,1,0:T(8,128)(2,1)S(1)} %bitcast.21), channel_id=1, source_target_pairs={{0,2},{1,3},{2,0},{3,1},{4,6},{5,7},{6,4},{7,5},{8,10},{9,11},{10,... | collective-permute-start | bytes 393224 | tf_op jit(solution)/shard_map/ppermute | solution.py:30
  47.9 7.0 %collective-permute-start.9 = (bf16[2,4,128,128]{3,2,1,0:T(8,128)(2,1)S(1)}, bf16[2,4,128,128]{3,2,1,0:T(8,128)(2,1)S(1)}, u32[]{:S(2)}, u32[]{:S(2)}) collective-permute-start(bf16[2,4,128,128]{3,2,1,0:T(8,128)(2,1)S(1)} %pad_maximum_fusion.1), channel_id=1, source_target_pairs={{0,1},{1,0},{2,3},{3,2},{4,5},{5,4},{6,7},{7,6},{8,9},{9,8},{10,11... | collective-permute-start | bytes 786440 | tf_op jit(solution)/shard_map/ppermute | solution.py:30
  48.0 7.1 %collective-permute-start.11 = (bf16[4,128,128]{2,1,0:T(8,128)(2,1)S(1)}, bf16[4,128,128]{2,1,0:T(8,128)(2,1)S(1)}, u32[]{:S(2)}, u32[]{:S(2)}) collective-permute-start(bf16[4,128,128]{2,1,0:T(8,128)(2,1)S(1)} %fusion.3), channel_id=1, source_target_pairs={{4,8},{12,16},{20,24},{8,4},{16,12},{24,20},{5,9},{13,17},{21,25},... | collective-permute-start | bytes 393224 | tf_op jit(solution)/shard_map/ppermute | solution.py:36
  48.7 10.8 %collective-permute-start.10 = (bf16[4,128,128]{2,1,0:T(8,128)(2,1)S(1)}, bf16[4,128,128]{2,1,0:T(8,128)(2,1)S(1)}, u32[]{:S(2)}, u32[]{:S(2)}) collective-permute-start(bf16[4,128,128]{2,1,0:T(8,128)(2,1)S(1)} %fusion.3), channel_id=1, source_target_pairs={{0,4},{4,0},{8,12},{12,8},{16,20},{20,16},{24,28},{28,24},{1,5},{5... | collective-permute-start | bytes 393224 | tf_op jit(solution)/shard_map/ppermute | solution.py:30
  61.3 1.4 %collective-permute-start.12 = (bf16[2,8,32,128]{3,2,1,0:T(8,128)(2,1)S(1)}, bf16[2,8,32,128]{3,2,1,0:T(8,128)(2,1)S(1)}, u32[]{:S(2)}, u32[]{:S(2)}) collective-permute-start(bf16[2,8,32,128]{3,2,1,0:T(8,128)(2,1)S(1)} %get-tuple-element.16), channel_id=1, source_target_pairs={{0,1},{1,0},{2,3},{3,2},{4,5},{5,4},{6,7},{7,6},{8,9},{9,8},{10,11... | collective-permute-start | bytes 393224 | tf_op jit(solution)/shard_map/ppermute | solution.py:30
  62.8 4.3 %collective-permute-start.13 = (bf16[1,8,32,128]{3,2,1,0:T(8,128)(2,1)S(1)}, bf16[1,8,32,128]{3,2,1,0:T(8,128)(2,1)S(1)}, u32[]{:S(2)}, u32[]{:S(2)}) collective-permute-start(bf16[1,8,32,128]{3,2,1,0:T(8,128)(2,1)S(1)} %slice.75), channel_id=1, source_target_pairs={{0,2},{1,3},{2,0},{3,1},{4,6},{5,7},{6,4},{7,5},{8,10},{9,11},{10,... | collective-permute-start | bytes 196616 | tf_op jit(solution)/shard_map/ppermute | solution.py:30

commit v2 on v1

--- a/solution.py
+++ b/solution.py
@@ -7,10 +7,13 @@
 from jax.experimental.pallas import tpu as pltpu
 from jax.sharding import PartitionSpec as P
 
+
 SWEEPS = 2
 NG = 8
 VMEM = pl.BlockSpec(memory_space=pltpu.VMEM)
 SMEM = pl.BlockSpec(memory_space=pltpu.SMEM)
+ANY = pl.BlockSpec(memory_space=pl.ANY)
+DIRECT = 3
 
 
 def call(kernel, ins, outs, scratch, flops, *args):
@@ -32,8 +35,10 @@
 
 def beside(x):
     size = lax.axis_size("elem")
-    across = [(i, i + 1) for i in range(1, size - 1, 2)]
-    return flip(x, "elem", 1), lax.ppermute(x, "elem", across + [(j, i) for i, j in across])
+    ring = [(i, (i + 1) % size) for i in range(size)]
+    before = lax.ppermute(x, "elem", ring)
+    after = lax.ppermute(x, "elem", [(j, i) for i, j in ring])
+    return before, after
 
 
 def scatter_sum(keep, send):
@@ -59,19 +64,14 @@
 
 
 def slot(pos_ref, element, count):
-    position = pos_ref[0]
-    offset = element - position * count
-    even = position % 2 == 0
-    below = jnp.where(even, 3 * count, 2 * count)
-    above = jnp.where(even, 0, count)
-    return offset + jnp.where(offset < 0, below, jnp.where(offset < count, 0, above))
-
-
-def fill(slabs, own, pair, across):
+    return element - (pos_ref[0] - 1) * count
+
+
+def fill(slabs, own, before, after):
     count = own.shape[0]
-    slabs[0:count] = own[...]
-    slabs[count : 2 * count] = pair[...]
-    slabs[2 * count : 3 * count] = across[...]
+    slabs[0:count] = before[...]
+    slabs[count : 2 * count] = own[...]
+    slabs[2 * count : 3 * count] = after[...]
 
 
 def split_rows(pos_ref, value, part_ref, keep_ref, send_ref, at):
@@ -87,9 +87,21 @@
             send_ref[r // 2, at] = chunk.astype(send_ref.dtype)
 
 
-def sweep_kernel(pos, nbrs, diag, blocks, own, pair, across, keep, send, slabs, part):
+def stage_kernel(diag, blocks, diag_out, blocks_out, sems):
+    count = diag.shape[0]
+    copies = []
+    for i in range(count):
+        copies.append(pltpu.make_async_copy(diag.at[i], diag_out.at[i], sems.at[2 * i]))
+        copies.append(pltpu.make_async_copy(blocks.at[i], blocks_out.at[i], sems.at[2 * i + 1]))
+    for copy in copies:
+        copy.start()
+    for copy in copies:
+        copy.wait()
+
+
+def sweep_kernel(pos, nbrs, diag, blocks, own, before, after, keep, send, slabs, part):
     count, faces = blocks.shape[0], blocks.shape[1]
-    fill(slabs, own, pair, across)
+    fill(slabs, own, before, after)
     for i in range(count):
         left = [diag[i]] + [blocks[i, k] for k in range(faces)]
         right = [own[i]] + [slabs[slot(pos, nbrs[i, k], count)] for k in range(faces)]
@@ -101,25 +113,28 @@
         split_rows(pos, y, part, keep, send, i)
 
 
-def couple_kernel(
-    pos, nbrs, agg, group, diag, blocks, every, pair, across, keep, send, slabs, part
-):
+def left_kernel(pos, diag, blocks, every, w):
     count, faces = blocks.shape[0], blocks.shape[1]
-    width = pair.shape[2]
-    fill(slabs, every.at[0], pair, across)
-    first = pos[0] * count
     for i in range(count):
         rows = [every[pos[1] ^ j, i] for j in range(every.shape[0])]
         left = [diag[i]] + [blocks[i, k] for k in range(faces)]
-        w = lax.dot_general(
+        w[i] = lax.dot_general(
             jnp.concatenate(rows, axis=0),
             jnp.concatenate(left, axis=1),
             (((0,), (0,)), ((), ())),
             preferred_element_type=jnp.float32,
-        ).astype(jnp.bfloat16)
+        ).astype(w.dtype)
+
+
+def couple_kernel(pos, nbrs, agg, group, w, own, before, after, keep, send, slabs, part):
+    count, width = own.shape[0], own.shape[2]
+    faces = w.shape[2] // own.shape[1] - 1
+    fill(slabs, own, before, after)
+    first = pos[0] * count
+    for i in range(count):
         own_agg = agg[first + i]
         own_group = group[own_agg]
-        right = [jnp.concatenate([slabs[i], slabs[i]], axis=1)]
+        right = [jnp.concatenate([own[i], own[i]], axis=1)]
         for k in range(faces):
             near = nbrs[i, k]
             near_agg = agg[near]
@@ -134,9 +149,35 @@
                     axis=1,
                 )
             )
-        t = jnp.dot(w, jnp.concatenate(right, axis=0), preferred_element_type=jnp.float32)
+        t = jnp.dot(w[i], jnp.concatenate(right, axis=0), preferred_element_type=jnp.float32)
         split_rows(pos, t[:, :width], part, keep, send, i)
         split_rows(pos, t[:, width:], part, keep, send, count + i)
+
+
+def merge_kernel(pos, agg, group, *refs):
+    raws, (coarse, last, send) = refs[:-3], refs[-3:]
+    count = raws[0].shape[0] // 2
+    owned, groups = coarse.shape[0], last.shape[0]
+    mine = [0.0] * owned
+    theirs = [0.0] * owned
+    level = [0.0] * groups
+    for k, raw in enumerate(raws):
+        source = (pos[0] ^ (2 * k)) * count
+        for i in range(count):
+            at = agg[source + i]
+            value = raw[i].astype(jnp.float32)
+            for j in range(owned):
+                mine[j] += jnp.where(at == pos[0] * owned + j, value, 0.0)
+                theirs[j] += jnp.where(at == (pos[0] ^ 1) * owned + j, value, 0.0)
+            value = raw[count + i].astype(jnp.float32)
+            for g in range(groups):
+                level[g] += jnp.where(group[at] == g, value, 0.0)
+    for j in range(owned):
+        coarse[j] = mine[j]
+        send[j] = theirs[j].astype(send.dtype)
+    for g in range(groups):
+        last[g] = level[g]
+        send[owned + g] = level[g].astype(send.dtype)
 
 
 def pack_kernel(pos, agg, total, out, sums):
@@ -171,7 +212,56 @@
     lax.fori_loop(0, parts.shape[0], one, 0)
 
 
-def body(diag, blocks, neighbours, damping, bases, agglomerate, group):
+def direct_tail(pos, agglomerate, group, total):
+    size = lax.axis_size("elem")
+    owned = group.shape[0] // size
+    _, part, width = total.shape
+    shape = jax.ShapeDtypeStruct
+    raw = total.astype(jnp.bfloat16)
+    raws = [raw]
+    for k in range(2, size, 2):
+        raws.append(flip(raw, "elem", k))
+    coarse, last, send = call(
+        merge_kernel,
+        [SMEM] * 3 + [VMEM] * len(raws),
+        [
+            shape((owned, part, width), jnp.float32),
+            shape((NG, part, width), jnp.float32),
+            shape((owned + NG, part, width), jnp.bfloat16),
+        ],
+        [],
+        1 << 20,
+        *(pos, agglomerate, group, *raws),
+    )
+    received = flip(send, "elem", 1)
+    return coarse + received[:owned], last + received[owned:]
+
+
+def routed_tail(pos, agglomerate, group, total):
+    size = lax.axis_size("elem")
+    owned = group.shape[0] // size
+    count, part, width = total.shape[0] // 2, total.shape[1], total.shape[2]
+    shape = jax.ShapeDtypeStruct
+    (parts,) = call(
+        pack_kernel,
+        [SMEM, SMEM, VMEM],
+        [shape((size, owned + count, part, width), jnp.bfloat16)],
+        [pltpu.VMEM((group.shape[0], part, width), jnp.float32)],
+        1 << 20,
+        *(pos, agglomerate, total),
+    )
+    parts = lax.all_to_all(parts, "elem", 0, 0, tiled=True)
+    return call(
+        functools.partial(finish_kernel, count=count),
+        [SMEM, SMEM, VMEM],
+        [shape((owned, part, width), jnp.float32), shape((NG, part, width), jnp.float32)],
+        [],
+        1 << 20,
+        *(agglomerate, group, parts),
+    )
+
+
+def steps(diag, blocks, neighbours, damping, bases, agglomerate, group):
     count, rows, width = bases.shape
     faces = neighbours.shape[1]
     ways = lax.axis_size("blk")
@@ -183,8 +273,16 @@
     flops = 2 * count * (faces + 1) * ways * rows * rows * width
 
     x = bases
-    pair, across = beside(x)
-    for _ in range(SWEEPS):
+    before, after = beside(x)
+    diag, blocks = call(
+        stage_kernel,
+        [ANY, ANY],
+        [shape(diag.shape, bf16), shape(blocks.shape, bf16)],
+        [pltpu.SemaphoreType.DMA((2 * count,))],
+        flops,
+        *(diag, blocks),
+    )
+    for sweep in range(SWEEPS):
         keep, send = call(
             sweep_kernel,
             [SMEM, SMEM] + [VMEM] * 5,
@@ -194,51 +292,44 @@
             ],
             [slabs, pltpu.VMEM((ways, rows, width), f32)],
             flops,
-            *(pos, neighbours, diag, blocks, x, pair, across),
+            *(pos, neighbours, diag, blocks, x, before, after),
         )
         total = scatter_sum(keep, send)
         x = (x.astype(f32) - damping[:, :, None] * total).astype(bf16)
-        pair, across = beside(x)
+        if sweep + 1 < SWEEPS:
+            before, after = beside(x)
 
     every = gathered(x)
+    before, after = beside(x)
+    (w,) = call(
+        left_kernel,
+        [SMEM] + [VMEM] * 3,
+        [shape((count, width, (faces + 1) * rows), bf16)],
+        [],
+        flops,
+        *(pos, diag, blocks, every),
+    )
     part = width // ways
     keep, send = call(
         couple_kernel,
-        [SMEM] * 4 + [VMEM] * 5,
+        [SMEM] * 4 + [VMEM] * 4,
         [
             shape((ways // 2, 2 * count, part, width), f32),
             shape((ways // 2, 2 * count, part, width), bf16),
         ],
         [slabs, pltpu.VMEM((ways, part, width), f32)],
         flops,
-        *(pos, neighbours, agglomerate, group, diag, blocks, every, pair, across),
+        *(pos, neighbours, agglomerate, group, w, x, before, after),
     )
     total = scatter_sum(keep, send)
-
-    owned = group.shape[0] // size
-    (parts,) = call(
-        pack_kernel,
-        [SMEM, SMEM, VMEM],
-        [shape((size, owned + count, part, width), bf16)],
-        [pltpu.VMEM((group.shape[0], part, width), f32)],
-        1 << 20,
-        *(pos, agglomerate, total),
-    )
-    parts = lax.all_to_all(parts, "elem", 0, 0, tiled=True)
-    coarse, last = call(
-        functools.partial(finish_kernel, count=count),
-        [SMEM, SMEM, VMEM],
-        [shape((owned, part, width), f32), shape((NG, part, width), f32)],
-        [],
-        1 << 20,
-        *(agglomerate, group, parts),
-    )
+    tail = direct_tail if size % 2 == 0 and size // 2 - 1 <= DIRECT else routed_tail
+    coarse, last = tail(pos, agglomerate, group, total)
     return x, coarse, last
 
 
 def solution(mesh):
     return jax.shard_map(
-        body,
+        steps,
         mesh=mesh,
         in_specs=(
             P("elem", None, "blk"),

time: 86.7 us -> 77.4 us (0.89)
  blocking collectives: 17.2 us -> 0 us
  waiting for transfers between devices: 29.1 us -> 33.8 us
  starting transfers between devices: 26.8 us -> 28.2 us
  other arithmetic: 0.61 us -> 1.91 us
    all_to_all x1 -> x0, blocking collectives: 17.2 us -> none  [body(): parts = lax.all_to_all(parts, 'elem', 0, 0, tiled=True)]
    ppermute x3 -> x6, starting transfers between devices: 1.99 us -> 15.7 us  [the longest x3 12.2 us: beside(): after = lax.ppermute(x, 'elem', [(j, i) for i, j in ring])]
    ppermute x11 -> x12, starting transfers between devices: 24.8 us -> 12.6 us  [flip(): lax.ppermute(x, axis, [(i, i ^ bit) for i in range(size) if i ^ bit < size])]
    ppermute x3 -> x6, waiting for transfers between devices: 0.01 us -> 6.98 us  [the longest x3 5.44 us: beside(): before = lax.ppermute(x, 'elem', ring)]
    ppermute x11 -> x12, waiting for transfers between devices: 29.1 us -> 26.8 us  [flip(): lax.ppermute(x, axis, [(i, i ^ bit) for i in range(size) if i ^ bit < size])]
    add x0 -> x2, other arithmetic: none -> 1.29 us  [direct_tail(): return (coarse + received[:owned], last + received[owned:])]
    pallas_call x5 -> x6, Pallas kernels: 7.28 us -> 7.62 us  [call(): pl.pallas_call(kernel, in_specs=ins, out_specs=[VMEM] * len(outs), out_sh...]
    unnamed x16 -> x20, local copies, waits for them, and re-layouts: 4.54 us -> 4.79 us
  transfers between devices with their start and end apart: 14 -> 18, of which waited for: 10 -> 15; matrix products, arithmetic and copies ran while one was open for 0% -> 0% of each run, Pallas kernels for 0% -> 3%
where the time goes in v2:
time: 77.4 us; the launch traced here: 77.2 us
  waiting for transfers between devices  33.8 us (44%)
  starting transfers between devices  28.2 us (36%)
  Pallas kernels  7.62 us (10%)
  local copies, waits for them, and re-layouts  4.86 us (6%)
  other arithmetic  1.91 us (2%)
  between operations  0.82 us (1%)
    ppermute x12, waiting for transfers between devices, flip(): lax.ppermute(x, axis, [(i, i ^ bit) for i in range(size) if i ^ bit < size])  26.8 us
    ppermute x12, starting transfers between devices, flip(): lax.ppermute(x, axis, [(i, i ^ bit) for i in range(size) if i ^ bit < size])  12.6 us
    ppermute x3, starting transfers between devices, beside(): after = lax.ppermute(x, 'elem', [(j, i) for i, j in ring])  12.2 us
    pallas_call x6, Pallas kernels, call(): pl.pallas_call(kernel, in_specs=ins, out_specs=[VMEM] * len(outs), out_sh...  7.62 us
    ppermute x3, waiting for transfers between devices, beside(): before = lax.ppermute(x, 'elem', ring)  5.44 us
    unnamed x20, local copies, waits for them, and re-layouts  4.79 us
    ppermute x3, starting transfers between devices, beside(): before = lax.ppermute(x, 'elem', ring)  3.51 us
  transfers between devices with their start and end apart: 18, of which 15 were waited for; matrix products, arithmetic and copies ran while one was open for 0% of the time, Pallas kernels for 3%

profile of v2, /device:TPU:0, one launch (start us, length us, event | category | flops | bytes accessed | tf_op | source)
XLA Modules:
  0.0 77.2 jit_solution(15998204132972667027)
XLA Ops:
  0.6 3.0 %collective-permute-start = (bf16[4,128,128]{2,1,0:T(8,128)(2,1)}, bf16[4,128,128]{2,1,0:T(8,128)(2,1)S(1)}, u32[]{:S(2)}, u32[]{:S(2)}) collective-permute-start(bf16[4,128,128]{2,1,0:T(8,128)(2,1)} %own.1), channel_id=1, source_target_pairs={{0,4},{4,8},{8,12},{12,16},{16,20},{20,24},{24,28},{28,0},{1,5},{5... | collective-permute-start | bytes 393224 | tf_op jit(solution)/shard_map/ppermute | solution.py:39
  3.7 3.1 %collective-permute-start.1 = (bf16[4,128,128]{2,1,0:T(8,128)(2,1)}, bf16[4,128,128]{2,1,0:T(8,128)(2,1)S(1)}, u32[]{:S(2)}, u32[]{:S(2)}) collective-permute-start(bf16[4,128,128]{2,1,0:T(8,128)(2,1)} %own.1), channel_id=1, source_target_pairs={{4,0},{8,4},{12,8},{16,12},{20,16},{24,20},{28,24},{0,28},{5,1},{9... | collective-permute-start | bytes 393224 | tf_op jit(solution)/shard_map/ppermute | solution.py:40
  6.8 1.9 %copy-done.2 = bf16[4,6,512,128]{3,2,1,0:T(8,128)(2,1)S(1)} copy-done((bf16[4,6,512,128]{3,2,1,0:T(8,128)(2,1)S(1)}, bf16[4,6,512,128]{3,2,1,0:T(8,128)(2,1)}, u32[]{:S(2)}) %copy-start.2) | copy-done | bytes 3145752
  8.6 1.0 %copy-done.4 = bf16[4,512,128]{2,1,0:T(8,128)(2,1)S(1)} copy-done((bf16[4,512,128]{2,1,0:T(8,128)(2,1)S(1)}, bf16[4,512,128]{2,1,0:T(8,128)(2,1)}, u32[]{:S(2)}) %copy-start.4) | copy-done | bytes 524312
  9.7 1.0 %shard_map.94 = (bf16[4,512,128]{2,1,0:T(8,128)(2,1)S(1)}, bf16[4,6,512,128]{3,2,1,0:T(8,128)(2,1)S(1)}) custom-call(bf16[4,512,128]{2,1,0:T(8,128)(2,1)S(1)} %copy-done.4, bf16[4,6,512,128]{3,2,1,0:T(8,128)(2,1)S(1)} %copy-done.2), custom_call_target="tpu_custom_call" | custom-call | flops 469762048 | bytes 4194304 | tf_op jit(solution)/shard_map/pallas_call | solution.py:20
  10.7 0.8 %copy-done = bf16[4,512,128]{2,1,0:T(8,128)(2,1)} copy-done((bf16[4,512,128]{2,1,0:T(8,128)(2,1)}, bf16[4,512,128]{2,1,0:T(8,128)(2,1)S(1)}, u32[]{:S(2)}) %copy-start) | copy-done | bytes 524312
  11.4 0.1 pad_add_fusion.pos
  11.5 0.1 collective-permute-done.1.after
  11.6 1.0 %copy-done.1 = bf16[4,512,128]{2,1,0:T(8,128)(2,1)S(1)} copy-done((bf16[4,512,128]{2,1,0:T(8,128)(2,1)S(1)}, bf16[4,512,128]{2,1,0:T(8,128)(2,1)}, u32[]{:S(2)}) %copy-start.1) | copy-done | bytes 524312
  12.7 1.7 %shard_map.95 = (f32[2,4,128,128]{3,2,1,0:T(8,128)S(1)}, bf16[2,4,128,128]{3,2,1,0:T(8,128)(2,1)S(1)}) custom-call(s32[2]{0:T(128)S(1)} %pad_add_fusion.pos, s32[4,6]{1,0:T(4,128)S(1)} %copy-done.6, bf16[4,512,128]{2,1,0:T(8,128)(2,1)S(1)} %copy-done.1, bf16[4,6,512,128]{3,2,1,0:T(8,128)(2,1)S(1)} %get-tuple-element.15.blocks, ...), custom_call_target="tpu_custom_call" | custom-call | flops 469762048 | bytes 4194304 | tf_op jit(solution)/shard_map/pallas_call | solution.py:20
  14.4 0.1 collective-permute-start.2
  14.5 1.5 %collective-permute-done.2 = bf16[2,4,128,128]{3,2,1,0:T(8,128)(2,1)S(1)} collective-permute-done((bf16[2,4,128,128]{3,2,1,0:T(8,128)(2,1)S(1)}, bf16[2,4,128,128]{3,2,1,0:T(8,128)(2,1)S(1)}, u32[]{:S(2)}, u32[]{:S(2)}) %collective-permute-start.2) | collective-permute-done | bytes 262176 | tf_op jit(solution)/shard_map/ppermute | solution.py:33
  16.1 1.6 %collective-permute-start.3 = (bf16[1,4,128,128]{3,2,1,0:T(8,128)(2,1)S(1)}, bf16[1,4,128,128]{3,2,1,0:T(8,128)(2,1)S(1)}, u32[]{:S(2)}, u32[]{:S(2)}) collective-permute-start(bf16[1,4,128,128]{3,2,1,0:T(8,128)(2,1)S(1)} %slice.88), channel_id=1, source_target_pairs={{0,2},{1,3},{2,0},{3,1},{4,6},{5,7},{6,4},{7,5},{8,10},{9,11},{10,... | collective-permute-start | bytes 393224 | tf_op jit(solution)/shard_map/ppermute | solution.py:33
  17.7 4.0 %collective-permute-done.3 = bf16[1,4,128,128]{3,2,1,0:T(8,128)(2,1)S(1)} collective-permute-done((bf16[1,4,128,128]{3,2,1,0:T(8,128)(2,1)S(1)}, bf16[1,4,128,128]{3,2,1,0:T(8,128)(2,1)S(1)}, u32[]{:S(2)}, u32[]{:S(2)}) %collective-permute-start.3) | collective-permute-done | bytes 131104 | tf_op jit(solution)/shard_map/ppermute | solution.py:33
  21.7 0.1 fusion.7.own
  21.9 0.3 collective-permute-start.4
  22.2 4.5 %collective-permute-start.5 = (bf16[4,128,128]{2,1,0:T(8,128)(2,1)S(1)}, bf16[4,128,128]{2,1,0:T(8,128)(2,1)S(1)}, u32[]{:S(2)}, u32[]{:S(2)}) collective-permute-start(bf16[4,128,128]{2,1,0:T(8,128)(2,1)S(1)} %fusion.7.own), channel_id=1, source_target_pairs={{4,0},{8,4},{12,8},{16,12},{20,16},{24,20},{28,24},{0,28},{5,1},{9... | collective-permute-start | bytes 393224 | tf_op jit(solution)/shard_map/ppermute | solution.py:40
  26.6 2.9 %collective-permute-done.4.before = bf16[4,128,128]{2,1,0:T(8,128)(2,1)S(1)} collective-permute-done((bf16[4,128,128]{2,1,0:T(8,128)(2,1)S(1)}, bf16[4,128,128]{2,1,0:T(8,128)(2,1)S(1)}, u32[]{:S(2)}, u32[]{:S(2)}) %collective-permute-start.4) | collective-permute-done | bytes 131104 | tf_op jit(solution)/shard_map/ppermute | solution.py:39
  29.6 0.8 %collective-permute-done.5.after = bf16[4,128,128]{2,1,0:T(8,128)(2,1)S(1)} collective-permute-done((bf16[4,128,128]{2,1,0:T(8,128)(2,1)S(1)}, bf16[4,128,128]{2,1,0:T(8,128)(2,1)S(1)}, u32[]{:S(2)}, u32[]{:S(2)}) %collective-permute-start.5) | collective-permute-done | bytes 131104 | tf_op jit(solution)/shard_map/ppermute | solution.py:40
  30.4 1.7 %shard_map.96 = (f32[2,4,128,128]{3,2,1,0:T(8,128)S(1)}, bf16[2,4,128,128]{3,2,1,0:T(8,128)(2,1)S(1)}) custom-call(s32[2]{0:T(128)S(1)} %pad_add_fusion.pos, s32[4,6]{1,0:T(4,128)S(1)} %copy-done.6, bf16[4,512,128]{2,1,0:T(8,128)(2,1)S(1)} %copy-done.1, bf16[4,6,512,128]{3,2,1,0:T(8,128)(2,1)S(1)} %get-tuple-element.15.blocks, ...), custom_call_target="tpu_custom_call" | custom-call | flops 469762048 | bytes 4194304 | tf_op jit(solution)/shard_map/pallas_call | solution.py:20
  32.1 0.1 collective-permute-start.6
  32.2 1.5 %collective-permute-done.6 = bf16[2,4,128,128]{3,2,1,0:T(8,128)(2,1)S(1)} collective-permute-done((bf16[2,4,128,128]{3,2,1,0:T(8,128)(2,1)S(1)}, bf16[2,4,128,128]{3,2,1,0:T(8,128)(2,1)S(1)}, u32[]{:S(2)}, u32[]{:S(2)}) %collective-permute-start.6) | collective-permute-done | bytes 262176 | tf_op jit(solution)/shard_map/ppermute | solution.py:33
  33.8 1.6 %collective-permute-start.7 = (bf16[1,4,128,128]{3,2,1,0:T(8,128)(2,1)S(1)}, bf16[1,4,128,128]{3,2,1,0:T(8,128)(2,1)S(1)}, u32[]{:S(2)}, u32[]{:S(2)}) collective-permute-start(bf16[1,4,128,128]{3,2,1,0:T(8,128)(2,1)S(1)} %slice.87), channel_id=1, source_target_pairs={{0,2},{1,3},{2,0},{3,1},{4,6},{5,7},{6,4},{7,5},{8,10},{9,11},{10,... | collective-permute-start | bytes 393224 | tf_op jit(solution)/shard_map/ppermute | solution.py:33
  35.4 4.0 %collective-permute-done.7 = bf16[1,4,128,128]{3,2,1,0:T(8,128)(2,1)S(1)} collective-permute-done((bf16[1,4,128,128]{3,2,1,0:T(8,128)(2,1)S(1)}, bf16[1,4,128,128]{3,2,1,0:T(8,128)(2,1)S(1)}, u32[]{:S(2)}, u32[]{:S(2)}) %collective-permute-start.7) | collective-permute-done | bytes 131104 | tf_op jit(solution)/shard_map/ppermute | solution.py:33
  39.4 0.1 fusion.3.own
  39.6 1.6 %collective-permute-start.8 = (bf16[1,4,128,128]{3,2,1,0:T(8,128)(2,1)S(1)}, bf16[1,4,128,128]{3,2,1,0:T(8,128)(2,1)S(1)}, u32[]{:S(2)}, u32[]{:S(2)}) collective-permute-start(bf16[1,4,128,128]{3,2,1,0:T(8,128)(2,1)S(1)} %bitcast.21), channel_id=1, source_target_pairs={{0,2},{1,3},{2,0},{3,1},{4,6},{5,7},{6,4},{7,5},{8,10},{9,11},{10,... | collective-permute-start | bytes 393224 | tf_op jit(solution)/shard_map/ppermute | solution.py:33
  41.2 3.4 %collective-permute-done.8 = bf16[1,4,128,128]{3,2,1,0:T(8,128)(2,1)S(1)} collective-permute-done((bf16[1,4,128,128]{3,2,1,0:T(8,128)(2,1)S(1)}, bf16[1,4,128,128]{3,2,1,0:T(8,128)(2,1)S(1)}, u32[]{:S(2)}, u32[]{:S(2)}) %collective-permute-start.8) | collective-permute-done | bytes 131104 | tf_op jit(solution)/shard_map/ppermute | solution.py:33
  44.6 0.1 collective-permute-start.9
  44.7 0.2 collective-permute-start.10
  44.9 4.6 %collective-permute-start.11 = (bf16[4,128,128]{2,1,0:T(8,128)(2,1)S(1)}, bf16[4,128,128]{2,1,0:T(8,128)(2,1)S(1)}, u32[]{:S(2)}, u32[]{:S(2)}) collective-permute-start(bf16[4,128,128]{2,1,0:T(8,128)(2,1)S(1)} %fusion.3.own), channel_id=1, source_target_pairs={{4,0},{8,4},{12,8},{16,12},{20,16},{24,20},{28,24},{0,28},{5,1},{9... | collective-permute-start | bytes 393224 | tf_op jit(solution)/shard_map/ppermute | solution.py:40
  49.6 1.3 %shard_map.97.w = bf16[4,128,896]{2,1,0:T(8,128)(2,1)S(1)} custom-call(s32[2]{0:T(128)S(1)} %pad_add_fusion.pos, bf16[4,512,128]{2,1,0:T(8,128)(2,1)S(1)} %copy-done.1, bf16[4,6,512,128]{3,2,1,0:T(8,128)(2,1)S(1)} %get-tuple-element.15.blocks, bf16[4,4,128,128]{3,2,1,0:T(8,128)(2,1)S(1)} %pad_maximum_fusion.every), custom_call_target="tpu_custom_call" | custom-call | flops 469762048 | bytes 4194304 | tf_op jit(solution)/shard_map/pallas_call | solution.py:20
  50.9 2.5 %collective-permute-done.10.before = bf16[4,128,128]{2,1,0:T(8,128)(2,1)S(1)} collective-permute-done((bf16[4,128,128]{2,1,0:T(8,128)(2,1)S(1)}, bf16[4,128,128]{2,1,0:T(8,128)(2,1)S(1)}, u32[]{:S(2)}, u32[]{:S(2)}) %collective-permute-start.10) | collective-permute-done | bytes 131104 | tf_op jit(solution)/shard_map/ppermute | solution.py:39
  53.4 0.6 collective-permute-done.11.after
  54.0 1.1 %shard_map.98 = (f32[2,8,32,128]{3,2,1,0:T(8,128)S(1)}, bf16[2,8,32,128]{3,2,1,0:T(8,128)(2,1)S(1)}) custom-call(s32[2]{0:T(128)S(1)} %pad_add_fusion.pos, s32[4,6]{1,0:T(4,128)S(1)} %copy-done.6, s32[32]{0:T(128)S(1)} %copy-done.7, s32[16]{0:T(128)S(1)} %copy-done.8, bf16[4,128,896]{2,1,0:T(8,128)(2,1)S(1)} %shard_map.97.w, ...), custom_call_target="tpu_custom_call" | custom-call | flops 469762048 | bytes 4194304 | tf_op jit(solution)/shard_map/pallas_call | solution.py:20
  55.1 0.1 collective-permute-start.12
  55.2 1.3 %collective-permute-done.12 = bf16[2,8,32,128]{3,2,1,0:T(8,128)(2,1)S(1)} collective-permute-done((bf16[2,8,32,128]{3,2,1,0:T(8,128)(2,1)S(1)}, bf16[2,8,32,128]{3,2,1,0:T(8,128)(2,1)S(1)}, u32[]{:S(2)}, u32[]{:S(2)}) %collective-permute-start.12) | collective-permute-done | bytes 131104 | tf_op jit(solution)/shard_map/ppermute | solution.py:33
  56.6 1.6 %collective-permute-start.13 = (bf16[1,8,32,128]{3,2,1,0:T(8,128)(2,1)S(1)}, bf16[1,8,32,128]{3,2,1,0:T(8,128)(2,1)S(1)}, u32[]{:S(2)}, u32[]{:S(2)}) collective-permute-start(bf16[1,8,32,128]{3,2,1,0:T(8,128)(2,1)S(1)} %slice.89), channel_id=1, source_target_pairs={{0,2},{1,3},{2,0},{3,1},{4,6},{5,7},{6,4},{7,5},{8,10},{9,11},{10,... | collective-permute-start | bytes 196616 | tf_op jit(solution)/shard_map/ppermute | solution.py:33
  58.2 2.7 %collective-permute-done.13 = bf16[1,8,32,128]{3,2,1,0:T(8,128)(2,1)S(1)} collective-permute-done((bf16[1,8,32,128]{3,2,1,0:T(8,128)(2,1)S(1)}, bf16[1,8,32,128]{3,2,1,0:T(8,128)(2,1)S(1)}, u32[]{:S(2)}, u32[]{:S(2)}) %collective-permute-start.13) | collective-permute-done | bytes 65568 | tf_op jit(solution)/shard_map/ppermute | solution.py:33
  61.0 1.5 %collective-permute-start.14 = (bf16[8,32,128]{2,1,0:T(8,128)(2,1)S(1)}, bf16[8,32,128]{2,1,0:T(8,128)(2,1)S(1)}, u32[]{:S(2)}, u32[]{:S(2)}) collective-permute-start(bf16[8,32,128]{2,1,0:T(8,128)(2,1)S(1)} %fusion.9.refs_0_), channel_id=1, source_target_pairs={{0,8},{4,12},{8,0},{12,4},{16,24},{20,28},{24,16},{28,20},{1,9},{5... | collective-permute-start | bytes 196616 | tf_op jit(solution)/shard_map/ppermute | solution.py:33
  62.5 2.0 %collective-permute-start.15 = (bf16[8,32,128]{2,1,0:T(8,128)(2,1)S(1)}, bf16[8,32,128]{2,1,0:T(8,128)(2,1)S(1)}, u32[]{:S(2)}, u32[]{:S(2)}) collective-permute-start(bf16[8,32,128]{2,1,0:T(8,128)(2,1)S(1)} %fusion.9.refs_0_), channel_id=1, source_target_pairs={{0,16},{4,20},{8,24},{12,28},{16,0},{20,4},{24,8},{28,12},{1,17},{... | collective-permute-start | bytes 196616 | tf_op jit(solution)/shard_map/ppermute | solution.py:33
  64.5 0.9 %collective-permute-start.16 = (bf16[8,32,128]{2,1,0:T(8,128)(2,1)S(1)}, bf16[8,32,128]{2,1,0:T(8,128)(2,1)S(1)}, u32[]{:S(2)}, u32[]{:S(2)}) collective-permute-start(bf16[8,32,128]{2,1,0:T(8,128)(2,1)S(1)} %fusion.9.refs_0_), channel_id=1, source_target_pairs={{0,24},{4,28},{8,16},{12,20},{16,8},{20,12},{24,0},{28,4},{1,25},{... | collective-permute-start | bytes 196616 | tf_op jit(solution)/shard_map/ppermute | solution.py:33
  65.5 3.6 %collective-permute-done.15.refs_2_ = bf16[8,32,128]{2,1,0:T(8,128)(2,1)S(1)} collective-permute-done((bf16[8,32,128]{2,1,0:T(8,128)(2,1)S(1)}, bf16[8,32,128]{2,1,0:T(8,128)(2,1)S(1)}, u32[]{:S(2)}, u32[]{:S(2)}) %collective-permute-start.15) | collective-permute-done | bytes 65568 | tf_op jit(solution)/shard_map/ppermute | solution.py:33
  69.1 1.5 %collective-permute-done.16.refs_3_ = bf16[8,32,128]{2,1,0:T(8,128)(2,1)S(1)} collective-permute-done((bf16[8,32,128]{2,1,0:T(8,128)(2,1)S(1)}, bf16[8,32,128]{2,1,0:T(8,128)(2,1)S(1)}, u32[]{:S(2)}, u32[]{:S(2)}) %collective-permute-start.16) | collective-permute-done | bytes 65568 | tf_op jit(solution)/shard_map/ppermute | solution.py:33
  70.6 0.8 %shard_map.99 = (f32[2,32,128]{2,1,0:T(8,128)S(1)}, f32[8,32,128]{2,1,0:T(8,128)S(1)}, bf16[10,32,128]{2,1,0:T(8,128)(2,1)S(1)}) custom-call(s32[2]{0:T(128)S(1)} %pad_add_fusion.pos, s32[32]{0:T(128)S(1)} %copy-done.7, s32[16]{0:T(128)S(1)} %copy-done.8, bf16[8,32,128]{2,1,0:T(8,128)(2,1)S(1)} %fusion.9.refs_0_, ...), custom_call_target="tpu_custom_call" | custom-call | flops 1048576 | bytes 4194304 | tf_op jit(solution)/shard_map/pallas_call | solution.py:20
  71.4 1.5 %collective-permute-start.17 = (bf16[10,32,128]{2,1,0:T(8,128)(2,1)S(1)}, bf16[10,32,128]{2,1,0:T(8,128)(2,1)S(1)}, u32[]{:S(2)}, u32[]{:S(2)}) collective-permute-start(bf16[10,32,128]{2,1,0:T(8,128)(2,1)S(1)} %get-tuple-element.23), channel_id=1, source_target_pairs={{0,4},{4,0},{8,12},{12,8},{16,20},{20,16},{24,28},{28,24},{1,5},{5... | collective-permute-start | bytes 245768 | tf_op jit(solution)/shard_map/ppermute | solution.py:33
  72.8 3.1 %collective-permute-done.17 = bf16[10,32,128]{2,1,0:T(8,128)(2,1)S(1)} collective-permute-done((bf16[10,32,128]{2,1,0:T(8,128)(2,1)S(1)}, bf16[10,32,128]{2,1,0:T(8,128)(2,1)S(1)}, u32[]{:S(2)}, u32[]{:S(2)}) %collective-permute-start.17) | collective-permute-done | bytes 81952 | tf_op jit(solution)/shard_map/ppermute | solution.py:33
  75.9 0.7 convert_add_fusion.3
  76.6 0.6 convert_add_fusion.4
  (29 shorter events, 0.4 us)
Async XLA Ops:
  0.6 10.9 %collective-permute-start = (bf16[4,128,128]{2,1,0:T(8,128)(2,1)}, bf16[4,128,128]{2,1,0:T(8,128)(2,1)S(1)}, u32[]{:S(2)}, u32[]{:S(2)}) collective-permute-start(bf16[4,128,128]{2,1,0:T(8,128)(2,1)} %own.1), channel_id=1, source_target_pairs={{0,4},{4,8},{8,12},{12,16},{16,20},{20,24},{24,28},{28,0},{1,5},{5... | collective-permute-start | bytes 393224 | tf_op jit(solution)/shard_map/ppermute | solution.py:39
  3.7 8.0 %collective-permute-start.1 = (bf16[4,128,128]{2,1,0:T(8,128)(2,1)}, bf16[4,128,128]{2,1,0:T(8,128)(2,1)S(1)}, u32[]{:S(2)}, u32[]{:S(2)}) collective-permute-start(bf16[4,128,128]{2,1,0:T(8,128)(2,1)} %own.1), channel_id=1, source_target_pairs={{4,0},{8,4},{12,8},{16,12},{20,16},{24,20},{28,24},{0,28},{5,1},{9... | collective-permute-start | bytes 393224 | tf_op jit(solution)/shard_map/ppermute | solution.py:40
  6.8 1.9 %copy-start.2 = (bf16[4,6,512,128]{3,2,1,0:T(8,128)(2,1)S(1)}, bf16[4,6,512,128]{3,2,1,0:T(8,128)(2,1)}, u32[]{:S(2)}) copy-start(bf16[4,6,512,128]{3,2,1,0:T(8,128)(2,1)} %blocks.1) | copy-start | bytes 9437188
  8.6 1.0 %copy-start.4 = (bf16[4,512,128]{2,1,0:T(8,128)(2,1)S(1)}, bf16[4,512,128]{2,1,0:T(8,128)(2,1)}, u32[]{:S(2)}) copy-start(bf16[4,512,128]{2,1,0:T(8,128)(2,1)} %diag.1) | copy-start | bytes 1572868
  9.7 2.0 %copy-start.5 = (bf16[4,128,128]{2,1,0:T(8,128)(2,1)S(1)}, bf16[4,128,128]{2,1,0:T(8,128)(2,1)}, u32[]{:S(2)}) copy-start(bf16[4,128,128]{2,1,0:T(8,128)(2,1)} %own.1) | copy-start | bytes 393220
  9.7 2.0 %copy-start.6 = (s32[4,6]{1,0:T(4,128)S(1)}, s32[4,6]{1,0:T(4,128)}, u32[]{:S(2)}) copy-start(s32[4,6]{1,0:T(4,128)} %nbrs.5) | copy-start | bytes 292
  10.7 0.8 %copy-start = (bf16[4,512,128]{2,1,0:T(8,128)(2,1)}, bf16[4,512,128]{2,1,0:T(8,128)(2,1)S(1)}, u32[]{:S(2)}) copy-start(bf16[4,512,128]{2,1,0:T(8,128)(2,1)S(1)} %get-tuple-element.14.diag) | copy-start | bytes 1572868
  11.4 10.3 %copy-start.9 = (f32[4,128]{1,0:T(4,128)S(1)}, f32[4,128]{1,0:T(4,128)}, u32[]{:S(2)}) copy-start(f32[4,128]{1,0:T(4,128)} %param.10) | copy-start | bytes 6148
  11.6 1.0 %copy-start.1 = (bf16[4,512,128]{2,1,0:T(8,128)(2,1)S(1)}, bf16[4,512,128]{2,1,0:T(8,128)(2,1)}, u32[]{:S(2)}) copy-start(bf16[4,512,128]{2,1,0:T(8,128)(2,1)} %copy-done) | copy-start | bytes 1572868
  14.4 1.6 %collective-permute-start.2 = (bf16[2,4,128,128]{3,2,1,0:T(8,128)(2,1)S(1)}, bf16[2,4,128,128]{3,2,1,0:T(8,128)(2,1)S(1)}, u32[]{:S(2)}, u32[]{:S(2)}) collective-permute-start(bf16[2,4,128,128]{3,2,1,0:T(8,128)(2,1)S(1)} %get-tuple-element.17), channel_id=1, source_target_pairs={{0,1},{1,0},{2,3},{3,2},{4,5},{5,4},{6,7},{7,6},{8,9},{9,8},{10,11... | collective-permute-start | bytes 786440 | tf_op jit(solution)/shard_map/ppermute | solution.py:33
  16.1 5.6 %collective-permute-start.3 = (bf16[1,4,128,128]{3,2,1,0:T(8,128)(2,1)S(1)}, bf16[1,4,128,128]{3,2,1,0:T(8,128)(2,1)S(1)}, u32[]{:S(2)}, u32[]{:S(2)}) collective-permute-start(bf16[1,4,128,128]{3,2,1,0:T(8,128)(2,1)S(1)} %slice.88), channel_id=1, source_target_pairs={{0,2},{1,3},{2,0},{3,1},{4,6},{5,7},{6,4},{7,5},{8,10},{9,11},{10,... | collective-permute-start | bytes 393224 | tf_op jit(solution)/shard_map/ppermute | solution.py:33
  21.9 7.7 %collective-permute-start.4 = (bf16[4,128,128]{2,1,0:T(8,128)(2,1)S(1)}, bf16[4,128,128]{2,1,0:T(8,128)(2,1)S(1)}, u32[]{:S(2)}, u32[]{:S(2)}) collective-permute-start(bf16[4,128,128]{2,1,0:T(8,128)(2,1)S(1)} %fusion.7.own), channel_id=1, source_target_pairs={{0,4},{4,8},{8,12},{12,16},{16,20},{20,24},{24,28},{28,0},{1,5},{5... | collective-permute-start | bytes 393224 | tf_op jit(solution)/shard_map/ppermute | solution.py:39
  22.2 8.2 %collective-permute-start.5 = (bf16[4,128,128]{2,1,0:T(8,128)(2,1)S(1)}, bf16[4,128,128]{2,1,0:T(8,128)(2,1)S(1)}, u32[]{:S(2)}, u32[]{:S(2)}) collective-permute-start(bf16[4,128,128]{2,1,0:T(8,128)(2,1)S(1)} %fusion.7.own), channel_id=1, source_target_pairs={{4,0},{8,4},{12,8},{16,12},{20,16},{24,20},{28,24},{0,28},{5,1},{9... | collective-permute-start | bytes 393224 | tf_op jit(solution)/shard_map/ppermute | solution.py:40
  32.1 1.6 %collective-permute-start.6 = (bf16[2,4,128,128]{3,2,1,0:T(8,128)(2,1)S(1)}, bf16[2,4,128,128]{3,2,1,0:T(8,128)(2,1)S(1)}, u32[]{:S(2)}, u32[]{:S(2)}) collective-permute-start(bf16[2,4,128,128]{3,2,1,0:T(8,128)(2,1)S(1)} %get-tuple-element.19), channel_id=1, source_target_pairs={{0,1},{1,0},{2,3},{3,2},{4,5},{5,4},{6,7},{7,6},{8,9},{9,8},{10,11... | collective-permute-start | bytes 786440 | tf_op jit(solution)/shard_map/ppermute | solution.py:33
  33.8 5.6 %collective-permute-start.7 = (bf16[1,4,128,128]{3,2,1,0:T(8,128)(2,1)S(1)}, bf16[1,4,128,128]{3,2,1,0:T(8,128)(2,1)S(1)}, u32[]{:S(2)}, u32[]{:S(2)}) collective-permute-start(bf16[1,4,128,128]{3,2,1,0:T(8,128)(2,1)S(1)} %slice.87), channel_id=1, source_target_pairs={{0,2},{1,3},{2,0},{3,1},{4,6},{5,7},{6,4},{7,5},{8,10},{9,11},{10,... | collective-permute-start | bytes 393224 | tf_op jit(solution)/shard_map/ppermute | solution.py:33
  39.6 14.5 %copy-start.3 = (bf16[4,128,128]{2,1,0:T(8,128)(2,1)}, bf16[4,128,128]{2,1,0:T(8,128)(2,1)S(1)}, u32[]{:S(2)}) copy-start(bf16[4,128,128]{2,1,0:T(8,128)(2,1)S(1)} %fusion.3.own) | copy-start | bytes 393220
  39.6 5.0 %collective-permute-start.8 = (bf16[1,4,128,128]{3,2,1,0:T(8,128)(2,1)S(1)}, bf16[1,4,128,128]{3,2,1,0:T(8,128)(2,1)S(1)}, u32[]{:S(2)}, u32[]{:S(2)}) collective-permute-start(bf16[1,4,128,128]{3,2,1,0:T(8,128)(2,1)S(1)} %bitcast.21), channel_id=1, source_target_pairs={{0,2},{1,3},{2,0},{3,1},{4,6},{5,7},{6,4},{7,5},{8,10},{9,11},{10,... | collective-permute-start | bytes 393224 | tf_op jit(solution)/shard_map/ppermute | solution.py:33
  44.6 4.9 %collective-permute-start.9 = (bf16[2,4,128,128]{3,2,1,0:T(8,128)(2,1)S(1)}, bf16[2,4,128,128]{3,2,1,0:T(8,128)(2,1)S(1)}, u32[]{:S(2)}, u32[]{:S(2)}) collective-permute-start(bf16[2,4,128,128]{3,2,1,0:T(8,128)(2,1)S(1)} %pad_maximum_fusion.1), channel_id=1, source_target_pairs={{0,1},{1,0},{2,3},{3,2},{4,5},{5,4},{6,7},{7,6},{8,9},{9,8},{10,11... | collective-permute-start | bytes 786440 | tf_op jit(solution)/shard_map/ppermute | solution.py:33
  44.7 8.7 %collective-permute-start.10 = (bf16[4,128,128]{2,1,0:T(8,128)(2,1)S(1)}, bf16[4,128,128]{2,1,0:T(8,128)(2,1)S(1)}, u32[]{:S(2)}, u32[]{:S(2)}) collective-permute-start(bf16[4,128,128]{2,1,0:T(8,128)(2,1)S(1)} %fusion.3.own), channel_id=1, source_target_pairs={{0,4},{4,8},{8,12},{12,16},{16,20},{20,24},{24,28},{28,0},{1,5},{5... | collective-permute-start | bytes 393224 | tf_op jit(solution)/shard_map/ppermute | solution.py:39
  44.9 9.2 %collective-permute-start.11 = (bf16[4,128,128]{2,1,0:T(8,128)(2,1)S(1)}, bf16[4,128,128]{2,1,0:T(8,128)(2,1)S(1)}, u32[]{:S(2)}, u32[]{:S(2)}) collective-permute-start(bf16[4,128,128]{2,1,0:T(8,128)(2,1)S(1)} %fusion.3.own), channel_id=1, source_target_pairs={{4,0},{8,4},{12,8},{16,12},{20,16},{24,20},{28,24},{0,28},{5,1},{9... | collective-permute-start | bytes 393224 | tf_op jit(solution)/shard_map/ppermute | solution.py:40
  49.5 4.5 %copy-start.7 = (s32[32]{0:T(128)S(1)}, s32[32]{0:T(128)}, u32[]{:S(2)}) copy-start(s32[32]{0:T(128)} %agg.3) | copy-start | bytes 388
  49.5 4.5 %copy-start.8 = (s32[16]{0:T(128)S(1)}, s32[16]{0:T(128)}, u32[]{:S(2)}) copy-start(s32[16]{0:T(128)} %group.3) | copy-start | bytes 196
  55.1 1.4 %collective-permute-start.12 = (bf16[2,8,32,128]{3,2,1,0:T(8,128)(2,1)S(1)}, bf16[2,8,32,128]{3,2,1,0:T(8,128)(2,1)S(1)}, u32[]{:S(2)}, u32[]{:S(2)}) collective-permute-start(bf16[2,8,32,128]{3,2,1,0:T(8,128)(2,1)S(1)} %get-tuple-element.21), channel_id=1, source_target_pairs={{0,1},{1,0},{2,3},{3,2},{4,5},{5,4},{6,7},{7,6},{8,9},{9,8},{10,11... | collective-permute-start | bytes 393224 | tf_op jit(solution)/shard_map/ppermute | solution.py:33
  56.6 4.3 %collective-permute-start.13 = (bf16[1,8,32,128]{3,2,1,0:T(8,128)(2,1)S(1)}, bf16[1,8,32,128]{3,2,1,0:T(8,128)(2,1)S(1)}, u32[]{:S(2)}, u32[]{:S(2)}) collective-permute-start(bf16[1,8,32,128]{3,2,1,0:T(8,128)(2,1)S(1)} %slice.89), channel_id=1, source_target_pairs={{0,2},{1,3},{2,0},{3,1},{4,6},{5,7},{6,4},{7,5},{8,10},{9,11},{10,... | collective-permute-start | bytes 196616 | tf_op jit(solution)/shard_map/ppermute | solution.py:33
  61.0 4.5 %collective-permute-start.14 = (bf16[8,32,128]{2,1,0:T(8,128)(2,1)S(1)}, bf16[8,32,128]{2,1,0:T(8,128)(2,1)S(1)}, u32[]{:S(2)}, u32[]{:S(2)}) collective-permute-start(bf16[8,32,128]{2,1,0:T(8,128)(2,1)S(1)} %fusion.9.refs_0_), channel_id=1, source_target_pairs={{0,8},{4,12},{8,0},{12,4},{16,24},{20,28},{24,16},{28,20},{1,9},{5... | collective-permute-start | bytes 196616 | tf_op jit(solution)/shard_map/ppermute | solution.py:33
  62.5 6.6 %collective-permute-start.15 = (bf16[8,32,128]{2,1,0:T(8,128)(2,1)S(1)}, bf16[8,32,128]{2,1,0:T(8,128)(2,1)S(1)}, u32[]{:S(2)}, u32[]{:S(2)}) collective-permute-start(bf16[8,32,128]{2,1,0:T(8,128)(2,1)S(1)} %fusion.9.refs_0_), channel_id=1, source_target_pairs={{0,16},{4,20},{8,24},{12,28},{16,0},{20,4},{24,8},{28,12},{1,17},{... | collective-permute-start | bytes 196616 | tf_op jit(solution)/shard_map/ppermute | solution.py:33
  64.5 6.1 %collective-permute-start.16 = (bf16[8,32,128]{2,1,0:T(8,128)(2,1)S(1)}, bf16[8,32,128]{2,1,0:T(8,128)(2,1)S(1)}, u32[]{:S(2)}, u32[]{:S(2)}) collective-permute-start(bf16[8,32,128]{2,1,0:T(8,128)(2,1)S(1)} %fusion.9.refs_0_), channel_id=1, source_target_pairs={{0,24},{4,28},{8,16},{12,20},{16,8},{20,12},{24,0},{28,4},{1,25},{... | collective-permute-start | bytes 196616 | tf_op jit(solution)/shard_map/ppermute | solution.py:33
  71.4 4.5 %collective-permute-start.17 = (bf16[10,32,128]{2,1,0:T(8,128)(2,1)S(1)}, bf16[10,32,128]{2,1,0:T(8,128)(2,1)S(1)}, u32[]{:S(2)}, u32[]{:S(2)}) collective-permute-start(bf16[10,32,128]{2,1,0:T(8,128)(2,1)S(1)} %get-tuple-element.23), channel_id=1, source_target_pairs={{0,4},{4,0},{8,12},{12,8},{16,20},{20,16},{24,28},{28,24},{1,5},{5... | collective-permute-start | bytes 245768 | tf_op jit(solution)/shard_map/ppermute | solution.py:33

commit v3 on v2

v3 whole, which is shorter than its diff:
```python
import functools

import jax
import jax.numpy as jnp
from jax import lax
from jax.experimental import pallas as pl
from jax.experimental.pallas import tpu as pltpu
from jax.sharding import PartitionSpec as P


SWEEPS = 2
NG = 8
VMEM = pl.BlockSpec(memory_space=pltpu.VMEM)
SMEM = pl.BlockSpec(memory_space=pltpu.SMEM)
ANY = pl.BlockSpec(memory_space=pl.ANY)
DIRECT = 3


def call(kernel, ins, outs, scratch, flops, *args, place=VMEM):
    return pl.pallas_call(
        kernel,
        in_specs=ins,
        out_specs=[place] * len(outs),
        out_shape=outs,
        scratch_shapes=scratch,
        compiler_params=pltpu.CompilerParams(vmem_limit_bytes=24 << 20),
        cost_estimate=pl.CostEstimate(flops=flops, bytes_accessed=4 << 20, transcendentals=0),
    )(*args)


def flip(x, axis, bit):
    size = lax.axis_size(axis)
    return lax.ppermute(x, axis, [(i, i ^ bit) for i in range(size) if i ^ bit < size])


def whole_pairs(target):
    size, ways = lax.axis_size("elem"), lax.axis_size("blk")
    pairs = []
    for p in range(size):
        for b in range(ways):
            q, c = target(p, b)
            inside = 0 <= q < size
            pairs.append((p * ways + b, q * ways + c if inside else p * ways + (b ^ 1)))
    return pairs


def beside(x):
    axes = ("elem", "blk")
    one = lax.ppermute(x, axes, whole_pairs(lambda p, b: (p ^ 1, b)))
    two = lax.ppermute(x, axes, whole_pairs(lambda p, b: (p - 1 + 2 * (p % 2), b)))
    return one, two


def swapped():
    return 1 - lax.axis_index("elem") % 2


def halved(keep, send):
    bit = 1
    while True:
        other = flip(send, "blk", bit)
        total = keep + other
        if total.shape[0] == 2:
            return total
        keep, send = total[0::2], total[1::2].astype(jnp.bfloat16)
        bit *= 2


def gathered(x, opposite):
    bit = lax.axis_size("blk") // 2
    parts = {0: x, bit: opposite}
    bit //= 2
    while bit:
        order = sorted(parts)
        other = flip(jnp.stack([parts[r] for r in order]), "blk", bit)
        for at, r in enumerate(order):
            parts[r + bit] = other[at]
        bit //= 2
    return jnp.stack([parts[r] for r in range(len(parts))])


def slot(pos_ref, element, count):
    offset = element - pos_ref[0] * count
    turn = jnp.where(offset < 0, 2 * count, jnp.where(offset < count, 0, -2 * count))
    return offset + count + pos_ref[2] * turn


def fill(slabs, pieces):
    at = 0
    for piece in pieces:
        slabs[at : at + piece.shape[0]] = piece[...]
        at += piece.shape[0]


def split_rows(pos_ref, value, part_ref, keep_ref, send_ref, at):
    chunks, rows = part_ref.shape[0], part_ref.shape[1]
    for j in range(chunks):
        part_ref[j] = value[j * rows : (j + 1) * rows]
    me = pos_ref[1]
    for r in range(chunks):
        chunk = part_ref[me ^ r]
        if r % 2 == 0:
            keep_ref[r // 2, at] = chunk
        else:
            send_ref[r // 2, at] = chunk.astype(send_ref.dtype)


def stage_kernel(_, diag, blocks, bases, diag_out, blocks_out, bases_out, sems):
    count = diag.shape[0]
    copies = [pltpu.make_async_copy(bases, bases_out, sems.at[2 * count])]
    for i in range(count):
        copies.append(pltpu.make_async_copy(diag.at[i], diag_out.at[i], sems.at[2 * i]))
        copies.append(pltpu.make_async_copy(blocks.at[i], blocks_out.at[i], sems.at[2 * i + 1]))
    for copy in copies:
        copy.start()
    for copy in copies:
        copy.wait()


def product(pos, nbrs, diag, blocks, slabs, out, parity):
    count, faces = blocks.shape[0], blocks.shape[1]
    rows = slabs.shape[1]
    for i in range(count):
        left = []
        for r in range(parity, 2 * out.shape[0], 2):
            cut = pl.ds(pl.multiple_of((pos[1] ^ r) * rows, rows), rows)
            line = [diag[i, cut, :]] + [blocks[i, k, cut, :] for k in range(faces)]
            left.append(jnp.concatenate(line, axis=1))
        right = [slabs[count + i]] + [slabs[slot(pos, nbrs[i, k], count)] for k in range(faces)]
        y = jnp.dot(
            jnp.concatenate(left, axis=0),
            jnp.concatenate(right, axis=0),
            preferred_element_type=jnp.float32,
        )
        for r in range(out.shape[0]):
            out[r, i] = y[r * rows : (r + 1) * rows].astype(out.dtype)


def send_kernel(pos, nbrs, diag, blocks, *refs):
    pieces, (send, slabs) = refs[:-2], refs[-2:]
    fill(slabs, pieces)
    product(pos, nbrs, diag, blocks, slabs, send, 1)


def keep_kernel(pos, nbrs, diag, blocks, slabs, keep):
    product(pos, nbrs, diag, blocks, slabs, keep, 0)


def left_kernel(pos, diag, blocks, every, w):
    count, faces = blocks.shape[0], blocks.shape[1]
    for i in range(count):
        rows = [every[pos[1] ^ j, i] for j in range(every.shape[0])]
        left = [diag[i]] + [blocks[i, k] for k in range(faces)]
        w[i] = lax.dot_general(
            jnp.concatenate(rows, axis=0),
            jnp.concatenate(left, axis=1),
            (((0,), (0,)), ((), ())),
            preferred_element_type=jnp.float32,
        ).astype(w.dtype)


def couple_kernel(pos, nbrs, agg, group, w, *refs):
    pieces, (keep, send, slabs, part) = refs[:-4], refs[-4:]
    count, width = w.shape[0], w.shape[1]
    faces = w.shape[2] // slabs.shape[1] - 1
    fill(slabs, pieces)
    first = pos[0] * count
    for i in range(count):
        own_agg = agg[first + i]
        own_group = group[own_agg]
        right = [jnp.concatenate([slabs[count + i]] * 2, axis=1)]
        for k in range(faces):
            near = nbrs[i, k]
            near_agg = agg[near]
            slab = slabs[slot(pos, near, count)]
            none = jnp.zeros_like(slab)
            right.append(
                jnp.concatenate(
                    [
                        jnp.where(near_agg == own_agg, slab, none),
                        jnp.where(group[near_agg] == own_group, slab, none),
                    ],
                    axis=1,
                )
            )
        t = jnp.dot(w[i], jnp.concatenate(right, axis=0), preferred_element_type=jnp.float32)
        split_rows(pos, t[:, :width], part, keep, send, i)
        split_rows(pos, t[:, width:], part, keep, send, count + i)


def merge_kernel(pos, agg, group, kept, opposite, pair, across, coarse, last, *sends):
    count = kept.shape[0] // 2
    owned, groups = coarse.shape[0], last.shape[0]
    sums = [[0.0] * owned for _ in range(len(sends) + 1)]
    level = [0.0] * groups
    for flipped in range(2):
        for i in range(2 * count):
            if flipped:
                value = pair[i].astype(jnp.float32) + across[i].astype(jnp.float32)
            else:
                value = kept[i] + opposite[i].astype(jnp.float32)
            at = agg[(pos[0] ^ flipped) * count + i % count]
            if i < count:
                for k in range(len(sums)):
                    for j in range(owned):
                        here = at == (pos[0] ^ (2 * k)) * owned + j
                        sums[k][j] += jnp.where(here, value, 0.0)
            else:
                for g in range(groups):
                    level[g] += jnp.where(group[at] == g, value, 0.0)
    for j in range(owned):
        coarse[j] = sums[0][j]
        for k, send in enumerate(sends):
            send[j] = sums[k + 1][j].astype(send.dtype)
    for g in range(groups):
        last[g] = level[g]
        for send in sends:
            send[owned + g] = level[g].astype(send.dtype)


def close_kernel(coarse, last, *refs):
    received, (coarse_hbm, last_hbm, coarse_sum, last_sum, sems) = refs[:-5], refs[-5:]
    owned = coarse.shape[0]
    total = coarse[...]
    for part in received:
        total += part[:owned].astype(jnp.float32)
    coarse_sum[...] = total
    total = last[...]
    for part in received:
        total += part[owned:].astype(jnp.float32)
    last_sum[...] = total
    first = pltpu.make_async_copy(coarse_sum, coarse_hbm, sems.at[0])
    second = pltpu.make_async_copy(last_sum, last_hbm, sems.at[1])
    first.start()
    second.start()
    first.wait()
    second.wait()


def pack_kernel(pos, agg, total, out, sums):
    count = total.shape[0] // 2
    owned = out.shape[1] - count
    sums[...] = jnp.zeros_like(sums)
    for i in range(count):
        at = agg[pos[0] * count + i]
        sums[at] = sums[at] + total[i]

    def one(dest, carry):
        for j in range(owned):
            out[dest, j] = sums[dest * owned + j].astype(out.dtype)
        out[dest, owned:] = total[count:].astype(out.dtype)
        return carry

    lax.fori_loop(0, out.shape[0], one, 0)


def finish_kernel(agg, group, parts, coarse, last, *, count):
    owned = coarse.shape[0]
    coarse[...] = jnp.zeros_like(coarse)
    last[...] = jnp.zeros_like(last)

    def one(source, carry):
        coarse[...] = coarse[...] + parts[source, :owned].astype(jnp.float32)
        for i in range(count):
            at = group[agg[source * count + i]]
            last[at] = last[at] + parts[source, owned + i].astype(jnp.float32)
        return carry

    lax.fori_loop(0, parts.shape[0], one, 0)


def direct_tail(pos, agglomerate, group, total):
    size, ways = lax.axis_size("elem"), lax.axis_size("blk")
    owned = group.shape[0] // size
    _, _, part, width = total.shape
    shape = jax.ShapeDtypeStruct
    bf16, f32 = jnp.bfloat16, jnp.float32
    half = ways // 2
    own, other = total[0].astype(bf16), total[1].astype(bf16)
    cross = [
        (p * ways + b, (p ^ 1) * ways + (b ^ half)) for p in range(size) for b in range(ways)
    ]
    opposite = flip(other, "blk", half)
    pair = flip(own, "elem", 1)
    across = lax.ppermute(other, ("elem", "blk"), cross)
    line = range(2, size, 2)
    packed = shape((owned + NG, part, width), bf16)
    coarse, last, *sends = call(
        merge_kernel,
        [SMEM] * 3 + [VMEM] * 4,
        [shape((owned, part, width), f32), shape((NG, part, width), f32)] + [packed] * len(line),
        [],
        1 << 20,
        *(pos, agglomerate, group, total[0], opposite, pair, across),
    )
    received = [flip(send, "elem", k) for k, send in zip(line, sends)]
    return call(
        close_kernel,
        [VMEM] * (2 + len(received)),
        [shape(coarse.shape, f32), shape(last.shape, f32)],
        [
            pltpu.VMEM(coarse.shape, f32),
            pltpu.VMEM(last.shape, f32),
            pltpu.SemaphoreType.DMA((2,)),
        ],
        1 << 20,
        *(coarse, last, *received),
        place=ANY,
    )


def routed_tail(pos, agglomerate, group, total):
    size = lax.axis_size("elem")
    owned = group.shape[0] // size
    total = total[0] + flip(total[1].astype(jnp.bfloat16), "blk", lax.axis_size("blk") // 2)
    count, part, width = total.shape[0] // 2, total.shape[1], total.shape[2]
    shape = jax.ShapeDtypeStruct
    (parts,) = call(
        pack_kernel,
        [SMEM, SMEM, VMEM],
        [shape((size, owned + count, part, width), jnp.bfloat16)],
        [pltpu.VMEM((group.shape[0], part, width), jnp.float32)],
        1 << 20,
        *(pos, agglomerate, total),
    )
    parts = lax.all_to_all(parts, "elem", 0, 0, tiled=True)
    return call(
        functools.partial(finish_kernel, count=count),
        [SMEM, SMEM, VMEM],
        [shape((owned, part, width), jnp.float32), shape((NG, part, width), jnp.float32)],
        [],
        1 << 20,
        *(agglomerate, group, parts),
    )


def steps(diag, blocks, neighbours, damping, bases, agglomerate, group):
    count, rows, width = bases.shape
    faces = neighbours.shape[1]
    ways = lax.axis_size("blk")
    size = lax.axis_size("elem")
    pos = jnp.stack([lax.axis_index("elem"), lax.axis_index("blk"), swapped()]).astype(jnp.int32)
    f32, bf16 = jnp.float32, jnp.bfloat16
    shape = jax.ShapeDtypeStruct
    flops = 2 * count * (faces + 1) * ways * rows * rows * width

    first, second = beside(bases)
    diag, blocks, x = call(
        stage_kernel,
        [SMEM] + [ANY] * 3,
        [shape(diag.shape, bf16), shape(blocks.shape, bf16), shape(bases.shape, bf16)],
        [pltpu.SemaphoreType.DMA((2 * count + 1,))],
        flops,
        *(pos, diag, blocks, bases),
    )
    half = ways // 2
    for sweep in range(SWEEPS):
        send, slabs = call(
            send_kernel,
            [SMEM, SMEM] + [VMEM] * 5,
            [
                shape((half, count, rows, width), bf16),
                shape((3 * count, rows, width), bf16),
            ],
            [],
            flops // 2,
            *(pos, neighbours, diag, blocks, first, x, second),
        )
        (keep,) = call(
            keep_kernel,
            [SMEM, SMEM] + [VMEM] * 3,
            [shape((half, count, rows, width), f32)],
            [],
            flops // 2,
            *(pos, neighbours, diag, blocks, slabs),
        )
        total = halved(keep, send)
        y = total[0] + flip(total[1].astype(bf16), "blk", half)
        x = (x.astype(f32) - damping[:, :, None] * y).astype(bf16)
        if sweep + 1 == SWEEPS:
            opposite = flip(x, "blk", half)
        first, second = beside(x)

    every = gathered(x, opposite)
    (w,) = call(
        left_kernel,
        [SMEM] + [VMEM] * 3,
        [shape((count, width, (faces + 1) * rows), bf16)],
        [],
        flops,
        *(pos, diag, blocks, every),
    )
    part = width // ways
    keep, send = call(
        couple_kernel,
        [SMEM] * 4 + [VMEM] * 4,
        [
            shape((ways // 2, 2 * count, part, width), f32),
            shape((ways // 2, 2 * count, part, width), bf16),
        ],
        [pltpu.VMEM((3 * count, rows, width), bf16), pltpu.VMEM((ways, part, width), f32)],
        flops,
        *(pos, neighbours, agglomerate, group, w, first, x, second),
    )
    total = halved(keep, send)
    tail = direct_tail if size % 2 == 0 and size // 2 - 1 <= DIRECT else routed_tail
    coarse, last = tail(pos, agglomerate, group, total)
    return x, coarse, last


def solution(mesh):
    return jax.shard_map(
        steps,
        mesh=mesh,
        in_specs=(
            P("elem", None, "blk"),
            P("elem", None, None, "blk"),
            P("elem", None),
            P("elem", "blk"),
            P("elem", "blk", None),
            P(),
            P(),
        ),
        out_specs=(P("elem", "blk", None), P("elem", "blk", None), P(None, "blk", None)),
        check_vma=False,
    )
```

time: 77.4 us -> 71.5 us (0.924)
  starting transfers between devices: 28.2 us -> 22.3 us
  Pallas kernels: 7.62 us -> 10.4 us
  other arithmetic: 1.91 us -> 0.6 us
  local copies, waits for them, and re-layouts: 4.86 us -> 3.96 us
    ppermute x6 -> x7, starting transfers between devices: 15.7 us -> 11 us  [the longest x3 8.37 us: beside(): one = lax.ppermute(x, axes, whole_pairs(lambda p, b: (p ^ 1, b)))]
    ppermute x12, waiting for transfers between devices: 26.8 us -> 23.3 us  [flip(): lax.ppermute(x, axis, [(i, i ^ bit) for i in range(size) if i ^ bit < size])]
    ppermute x6 -> x7, waiting for transfers between devices: 6.98 us -> 9.94 us  [the longest x3 9.93 us: beside(): one = lax.ppermute(x, axes, whole_pairs(lambda p, b: (p ^ 1, b)))]
    pallas_call x6 -> x9, Pallas kernels: 7.62 us -> 10.4 us  [call(): pl.pallas_call(kernel, in_specs=ins, out_specs=[place] * len(outs), out_s...]
    add x5 -> x3, other arithmetic: 1.45 us -> 0.15 us  [halved(): total = keep + other]
    ppermute x12, starting transfers between devices: 12.6 us -> 11.4 us  [flip(): lax.ppermute(x, axis, [(i, i ^ bit) for i in range(size) if i ^ bit < size])]
    unnamed x20 -> x16, local copies, waits for them, and re-layouts: 4.79 us -> 3.87 us
  transfers between devices with their start and end apart: 18 -> 19, of which waited for: 15 -> 13; matrix products, arithmetic and copies ran while one was open for 0% -> 0% of each run, Pallas kernels for 3% -> 8%
where the time goes in v3:
time: 71.5 us; the launch traced here: 71.3 us
  waiting for transfers between devices  33.2 us (46%)
  starting transfers between devices  22.3 us (31%)
  Pallas kernels  10.4 us (15%)
  local copies, waits for them, and re-layouts  3.96 us (6%)
  between operations  0.83 us (1%)
    ppermute x12, waiting for transfers between devices, flip(): lax.ppermute(x, axis, [(i, i ^ bit) for i in range(size) if i ^ bit < size])  23.3 us
    ppermute x12, starting transfers between devices, flip(): lax.ppermute(x, axis, [(i, i ^ bit) for i in range(size) if i ^ bit < size])  11.4 us
    pallas_call x9, Pallas kernels, call(): pl.pallas_call(kernel, in_specs=ins, out_specs=[place] * len(outs), out_s...  10.4 us
    ppermute x3, waiting for transfers between devices, beside(): one = lax.ppermute(x, axes, whole_pairs(lambda p, b: (p ^ 1, b)))  9.93 us
    ppermute x3, starting transfers between devices, beside(): one = lax.ppermute(x, axes, whole_pairs(lambda p, b: (p ^ 1, b)))  8.37 us
    unnamed x16, local copies, waits for them, and re-layouts  3.87 us
    ppermute x1, starting transfers between devices, direct_tail(): across = lax.ppermute(other, ('elem', 'blk'), cross)  2.44 us
  transfers between devices with their start and end apart: 19, of which 13 were waited for; matrix products, arithmetic and copies ran while one was open for 0% of the time, Pallas kernels for 8%

profile of v3, /device:TPU:0, one launch (start us, length us, event | category | flops | bytes accessed | tf_op | source)
XLA Modules:
  0.0 71.3 jit_solution(10692064524940704528)
XLA Ops:
  0.6 3.0 %collective-permute-start = (bf16[4,128,128]{2,1,0:T(8,128)(2,1)}, bf16[4,128,128]{2,1,0:T(8,128)(2,1)S(1)}, u32[]{:S(2)}, u32[]{:S(2)}) collective-permute-start(bf16[4,128,128]{2,1,0:T(8,128)(2,1)} %bases.1), channel_id=1, source_target_pairs={{0,4},{1,5},{2,6},{3,7},{4,0},{5,1},{6,2},{7,3},{8,12},{9,13},{10,... | collective-permute-start | bytes 393224 | tf_op jit(solution)/shard_map/ppermute | solution.py:49
  3.7 0.1 pad_add_fusion._.pos
  3.8 1.9 %copy-done = bf16[4,6,512,128]{3,2,1,0:T(8,128)(2,1)S(1)} copy-done((bf16[4,6,512,128]{3,2,1,0:T(8,128)(2,1)S(1)}, bf16[4,6,512,128]{3,2,1,0:T(8,128)(2,1)}, u32[]{:S(2)}) %copy-start) | copy-done | bytes 3145752
  5.6 1.0 %copy-done.2 = bf16[4,512,128]{2,1,0:T(8,128)(2,1)S(1)} copy-done((bf16[4,512,128]{2,1,0:T(8,128)(2,1)S(1)}, bf16[4,512,128]{2,1,0:T(8,128)(2,1)}, u32[]{:S(2)}) %copy-start.2) | copy-done | bytes 524312
  6.7 0.9 %copy-done.3 = bf16[4,128,128]{2,1,0:T(8,128)(2,1)S(1)} copy-done((bf16[4,128,128]{2,1,0:T(8,128)(2,1)S(1)}, bf16[4,128,128]{2,1,0:T(8,128)(2,1)}, u32[]{:S(2)}) %copy-start.3) | copy-done | bytes 131096
  7.6 1.7 %shard_map.94 = (bf16[4,512,128]{2,1,0:T(8,128)(2,1)S(1)}, bf16[4,6,512,128]{3,2,1,0:T(8,128)(2,1)S(1)}, bf16[4,128,128]{2,1,0:T(8,128)(2,1)S(1)}) custom-call(s32[3]{0:T(128)S(1)} %pad_add_fusion._.pos, bf16[4,512,128]{2,1,0:T(8,128)(2,1)S(1)} %copy-done.2, bf16[4,6,512,128]{3,2,1,0:T(8,128)(2,1)S(1)} %copy-done, bf16[4,128,128]{2,1,0:T(8,128)(2,1)S(1)} %copy-done.3), custom_call_target="tpu_custom_call" | custom-call | flops 469762048 | bytes 4194304 | tf_op jit(solution)/shard_map/pallas_call | solution.py:20
  9.3 0.3 collective-permute-done.refs_0_
  9.6 1.2 %shard_map.95 = (bf16[2,4,128,128]{3,2,1,0:T(8,128)(2,1)S(1)}, bf16[12,128,128]{2,1,0:T(8,128)(2,1)S(1)}) custom-call(s32[3]{0:T(128)S(1)} %pad_add_fusion._.pos, s32[4,6]{1,0:T(4,128)S(1)} %copy-done.4, bf16[4,512,128]{2,1,0:T(8,128)(2,1)S(1)} %get-tuple-element.20.diag, bf16[4,6,512,128]{3,2,1,0:T(8,128)(2,1)S(1)} %get-tuple-element.21.blocks, ...), custom_call_target="tpu_custom_call" | custom-call | flops 234881024 | bytes 4194304 | tf_op jit(solution)/shard_map/pallas_call | solution.py:20
  10.8 0.3 collective-permute-start.2
  11.1 1.2 %shard_map.96 = f32[2,4,128,128]{3,2,1,0:T(8,128)S(1)} custom-call(s32[3]{0:T(128)S(1)} %pad_add_fusion._.pos, s32[4,6]{1,0:T(4,128)S(1)} %copy-done.4, bf16[4,512,128]{2,1,0:T(8,128)(2,1)S(1)} %get-tuple-element.20.diag, bf16[4,6,512,128]{3,2,1,0:T(8,128)(2,1)S(1)} %get-tuple-element.21.blocks, bf16[12,128,128]{2,1,0:T(8,128)(2,1)S(1)} %get-tuple-element.22.slabs), custom_call_target="tpu_custom_call" | custom-call | flops 234881024 | bytes 4194304 | tf_op jit(solution)/shard_map/pallas_call | solution.py:20
  12.3 0.1 collective-permute-done.2
  12.4 0.1 convert_add_fusion.1
  12.5 1.6 %collective-permute-start.3 = (bf16[4,128,128]{2,1,0:T(8,128)(2,1)S(1)}, bf16[4,128,128]{2,1,0:T(8,128)(2,1)S(1)}, u32[]{:S(2)}, u32[]{:S(2)}) collective-permute-start(bf16[4,128,128]{2,1,0:T(8,128)(2,1)S(1)} %fusion.8), channel_id=1, source_target_pairs={{0,2},{1,3},{2,0},{3,1},{4,6},{5,7},{6,4},{7,5},{8,10},{9,11},{10,... | collective-permute-start | bytes 393224 | tf_op jit(solution)/shard_map/ppermute | solution.py:33
  14.1 4.2 %collective-permute-done.3 = bf16[4,128,128]{2,1,0:T(8,128)(2,1)S(1)} collective-permute-done((bf16[4,128,128]{2,1,0:T(8,128)(2,1)S(1)}, bf16[4,128,128]{2,1,0:T(8,128)(2,1)S(1)}, u32[]{:S(2)}, u32[]{:S(2)}) %collective-permute-start.3) | collective-permute-done | bytes 131104 | tf_op jit(solution)/shard_map/ppermute | solution.py:33
  18.2 0.1 fusion.7.refs_1_
  18.4 2.8 %collective-permute-start.4 = (bf16[4,128,128]{2,1,0:T(8,128)(2,1)S(1)}, bf16[4,128,128]{2,1,0:T(8,128)(2,1)S(1)}, u32[]{:S(2)}, u32[]{:S(2)}) collective-permute-start(bf16[4,128,128]{2,1,0:T(8,128)(2,1)S(1)} %fusion.7.refs_1_), channel_id=1, source_target_pairs={{0,4},{1,5},{2,6},{3,7},{4,0},{5,1},{6,2},{7,3},{8,12},{9,13},{10,... | collective-permute-start | bytes 393224 | tf_op jit(solution)/shard_map/ppermute | solution.py:49
  21.2 5.1 %collective-permute-done.4.refs_0_ = bf16[4,128,128]{2,1,0:T(8,128)(2,1)S(1)} collective-permute-done((bf16[4,128,128]{2,1,0:T(8,128)(2,1)S(1)}, bf16[4,128,128]{2,1,0:T(8,128)(2,1)S(1)}, u32[]{:S(2)}, u32[]{:S(2)}) %collective-permute-start.4) | collective-permute-done | bytes 131104 | tf_op jit(solution)/shard_map/ppermute | solution.py:49
  26.2 1.2 %shard_map.97 = (bf16[2,4,128,128]{3,2,1,0:T(8,128)(2,1)S(1)}, bf16[12,128,128]{2,1,0:T(8,128)(2,1)S(1)}) custom-call(s32[3]{0:T(128)S(1)} %pad_add_fusion._.pos, s32[4,6]{1,0:T(4,128)S(1)} %copy-done.4, bf16[4,512,128]{2,1,0:T(8,128)(2,1)S(1)} %get-tuple-element.20.diag, bf16[4,6,512,128]{3,2,1,0:T(8,128)(2,1)S(1)} %get-tuple-element.21.blocks, ...), custom_call_target="tpu_custom_call" | custom-call | flops 234881024 | bytes 4194304 | tf_op jit(solution)/shard_map/pallas_call | solution.py:20
  27.5 0.1 collective-permute-start.6
  27.5 1.2 %shard_map.98 = f32[2,4,128,128]{3,2,1,0:T(8,128)S(1)} custom-call(s32[3]{0:T(128)S(1)} %pad_add_fusion._.pos, s32[4,6]{1,0:T(4,128)S(1)} %copy-done.4, bf16[4,512,128]{2,1,0:T(8,128)(2,1)S(1)} %get-tuple-element.20.diag, bf16[4,6,512,128]{3,2,1,0:T(8,128)(2,1)S(1)} %get-tuple-element.21.blocks, bf16[12,128,128]{2,1,0:T(8,128)(2,1)S(1)} %get-tuple-element.24.slabs), custom_call_target="tpu_custom_call" | custom-call | flops 234881024 | bytes 4194304 | tf_op jit(solution)/shard_map/pallas_call | solution.py:20
  28.8 0.3 collective-permute-done.6
  29.1 0.1 convert_add_fusion
  29.2 1.6 %collective-permute-start.7 = (bf16[4,128,128]{2,1,0:T(8,128)(2,1)S(1)}, bf16[4,128,128]{2,1,0:T(8,128)(2,1)S(1)}, u32[]{:S(2)}, u32[]{:S(2)}) collective-permute-start(bf16[4,128,128]{2,1,0:T(8,128)(2,1)S(1)} %fusion.9), channel_id=1, source_target_pairs={{0,2},{1,3},{2,0},{3,1},{4,6},{5,7},{6,4},{7,5},{8,10},{9,11},{10,... | collective-permute-start | bytes 393224 | tf_op jit(solution)/shard_map/ppermute | solution.py:33
  30.7 4.1 %collective-permute-done.7 = bf16[4,128,128]{2,1,0:T(8,128)(2,1)S(1)} collective-permute-done((bf16[4,128,128]{2,1,0:T(8,128)(2,1)S(1)}, bf16[4,128,128]{2,1,0:T(8,128)(2,1)S(1)}, u32[]{:S(2)}, u32[]{:S(2)}) %collective-permute-start.7) | collective-permute-done | bytes 131104 | tf_op jit(solution)/shard_map/ppermute | solution.py:33
  34.8 0.1 fusion.3.refs_1_
  35.0 1.6 %collective-permute-start.8 = (bf16[4,128,128]{2,1,0:T(8,128)(2,1)S(1)}, bf16[4,128,128]{2,1,0:T(8,128)(2,1)S(1)}, u32[]{:S(2)}, u32[]{:S(2)}) collective-permute-start(bf16[4,128,128]{2,1,0:T(8,128)(2,1)S(1)} %fusion.3.refs_1_), channel_id=1, source_target_pairs={{0,2},{1,3},{2,0},{3,1},{4,6},{5,7},{6,4},{7,5},{8,10},{9,11},{10,... | collective-permute-start | bytes 393224 | tf_op jit(solution)/shard_map/ppermute | solution.py:33
  36.5 3.5 %collective-permute-done.8 = bf16[4,128,128]{2,1,0:T(8,128)(2,1)S(1)} collective-permute-done((bf16[4,128,128]{2,1,0:T(8,128)(2,1)S(1)}, bf16[4,128,128]{2,1,0:T(8,128)(2,1)S(1)}, u32[]{:S(2)}, u32[]{:S(2)}) %collective-permute-start.8) | collective-permute-done | bytes 131104 | tf_op jit(solution)/shard_map/ppermute | solution.py:33
  40.0 0.1 collective-permute-start.9
  40.1 2.5 %collective-permute-start.10 = (bf16[4,128,128]{2,1,0:T(8,128)(2,1)S(1)}, bf16[4,128,128]{2,1,0:T(8,128)(2,1)S(1)}, u32[]{:S(2)}, u32[]{:S(2)}) collective-permute-start(bf16[4,128,128]{2,1,0:T(8,128)(2,1)S(1)} %fusion.3.refs_1_), channel_id=1, source_target_pairs={{0,4},{1,5},{2,6},{3,7},{4,0},{5,1},{6,2},{7,3},{8,12},{9,13},{10,... | collective-permute-start | bytes 393224 | tf_op jit(solution)/shard_map/ppermute | solution.py:49
  42.7 0.2 collective-permute-start.11
  42.9 0.1 pad_maximum_fusion.every
  42.9 1.3 %shard_map.99.w = bf16[4,128,896]{2,1,0:T(8,128)(2,1)S(1)} custom-call(s32[3]{0:T(128)S(1)} %pad_add_fusion._.pos, bf16[4,512,128]{2,1,0:T(8,128)(2,1)S(1)} %get-tuple-element.20.diag, bf16[4,6,512,128]{3,2,1,0:T(8,128)(2,1)S(1)} %get-tuple-element.21.blocks, bf16[4,4,128,128]{3,2,1,0:T(8,128)(2,1)S(1)} %pad_maximum_fusion.every), custom_call_target="tpu_custom_call" | custom-call | flops 469762048 | bytes 4194304 | tf_op jit(solution)/shard_map/pallas_call | solution.py:20
  44.2 4.6 %collective-permute-done.10.refs_0_ = bf16[4,128,128]{2,1,0:T(8,128)(2,1)S(1)} collective-permute-done((bf16[4,128,128]{2,1,0:T(8,128)(2,1)S(1)}, bf16[4,128,128]{2,1,0:T(8,128)(2,1)S(1)}, u32[]{:S(2)}, u32[]{:S(2)}) %collective-permute-start.10) | collective-permute-done | bytes 131104 | tf_op jit(solution)/shard_map/ppermute | solution.py:49
  48.8 1.1 %shard_map.100 = (f32[2,8,32,128]{3,2,1,0:T(8,128)S(1)}, bf16[2,8,32,128]{3,2,1,0:T(8,128)(2,1)S(1)}) custom-call(s32[3]{0:T(128)S(1)} %pad_add_fusion._.pos, s32[4,6]{1,0:T(4,128)S(1)} %copy-done.4, s32[32]{0:T(128)S(1)} %copy-done.5, s32[16]{0:T(128)S(1)} %copy-done.6, bf16[4,128,896]{2,1,0:T(8,128)(2,1)S(1)} %shard_map.99.w, ...), custom_call_target="tpu_custom_call" | custom-call | flops 469762048 | bytes 4194304 | tf_op jit(solution)/shard_map/pallas_call | solution.py:20
  49.9 0.1 collective-permute-start.12
  50.0 1.3 %collective-permute-done.12 = bf16[2,8,32,128]{3,2,1,0:T(8,128)(2,1)S(1)} collective-permute-done((bf16[2,8,32,128]{3,2,1,0:T(8,128)(2,1)S(1)}, bf16[2,8,32,128]{3,2,1,0:T(8,128)(2,1)S(1)}, u32[]{:S(2)}, u32[]{:S(2)}) %collective-permute-start.12) | collective-permute-done | bytes 131104 | tf_op jit(solution)/shard_map/ppermute | solution.py:33
  51.4 1.6 %collective-permute-start.13 = (bf16[8,32,128]{2,1,0:T(8,128)(2,1)S(1)}, bf16[8,32,128]{2,1,0:T(8,128)(2,1)S(1)}, u32[]{:S(2)}, u32[]{:S(2)}) collective-permute-start(bf16[8,32,128]{2,1,0:T(8,128)(2,1)S(1)} %get-tuple-element.36), channel_id=1, source_target_pairs={{0,2},{1,3},{2,0},{3,1},{4,6},{5,7},{6,4},{7,5},{8,10},{9,11},{10,... | collective-permute-start | bytes 196616 | tf_op jit(solution)/shard_map/ppermute | solution.py:33
  53.0 2.4 %collective-permute-start.15 = (bf16[8,32,128]{2,1,0:T(8,128)(2,1)S(1)}, bf16[8,32,128]{2,1,0:T(8,128)(2,1)S(1)}, u32[]{:S(2)}, u32[]{:S(2)}) collective-permute-start(bf16[8,32,128]{2,1,0:T(8,128)(2,1)S(1)} %get-tuple-element.36), channel_id=1, source_target_pairs={{0,6},{1,7},{2,4},{3,5},{4,2},{5,3},{6,0},{7,1},{8,14},{9,15},{10,... | collective-permute-start | bytes 196616 | tf_op jit(solution)/shard_map/ppermute | solution.py:285
  55.4 0.1 collective-permute-start.14
  55.5 0.2 collective-permute-done.13.opposite
  55.8 4.0 %collective-permute-done.14.pair = bf16[8,32,128]{2,1,0:T(8,128)(2,1)S(1)} collective-permute-done((bf16[8,32,128]{2,1,0:T(8,128)(2,1)S(1)}, bf16[8,32,128]{2,1,0:T(8,128)(2,1)S(1)}, u32[]{:S(2)}, u32[]{:S(2)}) %collective-permute-start.14) | collective-permute-done | bytes 65568 | tf_op jit(solution)/shard_map/ppermute | solution.py:33
  59.7 0.7 %shard_map.101 = (f32[2,32,128]{2,1,0:T(8,128)S(1)}, f32[8,32,128]{2,1,0:T(8,128)S(1)}, bf16[10,32,128]{2,1,0:T(8,128)(2,1)S(1)}, bf16[10,32,128]{2,1,0:T(8,128)(2,1)S(1)}, bf16[10,32,128]{2,1,0:T(8,128)(2,1)S(1)}) custom-call(s32[3]{0:T(128)S(1)} %pad_add_fusion._.pos, s32[32]{0:T(128)S(1)} %copy-done.5, s32[16]{0:T(128)S(1)} %copy-done.6, ...), custom_call_target="tpu_custom_call" | custom-call | flops 1048576 | bytes 4194304 | tf_op jit(solution)/shard_map/pallas_call | solution.py:20
  60.5 1.6 %collective-permute-start.16 = (bf16[10,32,128]{2,1,0:T(8,128)(2,1)S(1)}, bf16[10,32,128]{2,1,0:T(8,128)(2,1)S(1)}, u32[]{:S(2)}, u32[]{:S(2)}) collective-permute-start(bf16[10,32,128]{2,1,0:T(8,128)(2,1)S(1)} %get-tuple-element.30), channel_id=1, source_target_pairs={{0,8},{4,12},{8,0},{12,4},{16,24},{20,28},{24,16},{28,20},{1,9},{5... | collective-permute-start | bytes 245768 | tf_op jit(solution)/shard_map/ppermute | solution.py:33
  62.1 1.9 %collective-permute-start.17 = (bf16[10,32,128]{2,1,0:T(8,128)(2,1)S(1)}, bf16[10,32,128]{2,1,0:T(8,128)(2,1)S(1)}, u32[]{:S(2)}, u32[]{:S(2)}) collective-permute-start(bf16[10,32,128]{2,1,0:T(8,128)(2,1)S(1)} %get-tuple-element.31), channel_id=1, source_target_pairs={{0,16},{4,20},{8,24},{12,28},{16,0},{20,4},{24,8},{28,12},{1,17},{... | collective-permute-start | bytes 245768 | tf_op jit(solution)/shard_map/ppermute | solution.py:33
  64.0 0.9 %collective-permute-start.18 = (bf16[10,32,128]{2,1,0:T(8,128)(2,1)S(1)}, bf16[10,32,128]{2,1,0:T(8,128)(2,1)S(1)}, u32[]{:S(2)}, u32[]{:S(2)}) collective-permute-start(bf16[10,32,128]{2,1,0:T(8,128)(2,1)S(1)} %get-tuple-element.32), channel_id=1, source_target_pairs={{0,24},{4,28},{8,16},{12,20},{16,8},{20,12},{24,0},{28,4},{1,25},{... | collective-permute-start | bytes 245768 | tf_op jit(solution)/shard_map/ppermute | solution.py:33
  64.9 0.9 %collective-permute-done.16.refs_0_ = bf16[10,32,128]{2,1,0:T(8,128)(2,1)S(1)} collective-permute-done((bf16[10,32,128]{2,1,0:T(8,128)(2,1)S(1)}, bf16[10,32,128]{2,1,0:T(8,128)(2,1)S(1)}, u32[]{:S(2)}, u32[]{:S(2)}) %collective-permute-start.16) | collective-permute-done | bytes 81952 | tf_op jit(solution)/shard_map/ppermute | solution.py:33
  65.8 4.8 %collective-permute-done.17.refs_1_ = bf16[10,32,128]{2,1,0:T(8,128)(2,1)S(1)} collective-permute-done((bf16[10,32,128]{2,1,0:T(8,128)(2,1)S(1)}, bf16[10,32,128]{2,1,0:T(8,128)(2,1)S(1)}, u32[]{:S(2)}, u32[]{:S(2)}) %collective-permute-start.17) | collective-permute-done | bytes 81952 | tf_op jit(solution)/shard_map/ppermute | solution.py:33
  70.6 0.7 %shard_map.102 = (f32[2,32,128]{2,1,0:T(8,128)}, f32[8,32,128]{2,1,0:T(8,128)}) custom-call(f32[2,32,128]{2,1,0:T(8,128)S(1)} %get-tuple-element.28.coarse, f32[8,32,128]{2,1,0:T(8,128)S(1)} %get-tuple-element.29.last, bf16[10,32,128]{2,1,0:T(8,128)(2,1)S(1)} %collective-permute-done.16.refs_0_, bf16[10,32,128]{2,1,0:T(8,128)(2,1)S(1)} %collective-permute-done.17.refs_1_, ...), custom_call_target="tpu_custom_call" | custom-call | flops 1048576 | bytes 4194304 | tf_op jit(solution)/shard_map/pallas_call | solution.py:20
  (28 shorter events, 0.2 us)
Async XLA Ops:
  0.6 8.9 %copy-start.4 = (s32[4,6]{1,0:T(4,128)S(1)}, s32[4,6]{1,0:T(4,128)}, u32[]{:S(2)}) copy-start(s32[4,6]{1,0:T(4,128)} %nbrs.9) | copy-start | bytes 292
  0.6 8.9 %collective-permute-start = (bf16[4,128,128]{2,1,0:T(8,128)(2,1)}, bf16[4,128,128]{2,1,0:T(8,128)(2,1)S(1)}, u32[]{:S(2)}, u32[]{:S(2)}) collective-permute-start(bf16[4,128,128]{2,1,0:T(8,128)(2,1)} %bases.1), channel_id=1, source_target_pairs={{0,4},{1,5},{2,6},{3,7},{4,0},{5,1},{6,2},{7,3},{8,12},{9,13},{10,... | collective-permute-start | bytes 393224 | tf_op jit(solution)/shard_map/ppermute | solution.py:49
  3.7 5.9 %collective-permute-start.1 = (bf16[4,128,128]{2,1,0:T(8,128)(2,1)}, bf16[4,128,128]{2,1,0:T(8,128)(2,1)S(1)}, u32[]{:S(2)}, u32[]{:S(2)}) collective-permute-start(bf16[4,128,128]{2,1,0:T(8,128)(2,1)} %bases.1), channel_id=1, source_target_pairs={{0,1},{1,0},{2,3},{3,2},{4,8},{5,9},{6,10},{7,11},{8,4},{9,5},{10,... | collective-permute-start | bytes 393224 | tf_op jit(solution)/shard_map/ppermute | solution.py:50
  3.8 1.9 %copy-start = (bf16[4,6,512,128]{3,2,1,0:T(8,128)(2,1)S(1)}, bf16[4,6,512,128]{3,2,1,0:T(8,128)(2,1)}, u32[]{:S(2)}) copy-start(bf16[4,6,512,128]{3,2,1,0:T(8,128)(2,1)} %blocks.1) | copy-start | bytes 9437188
  5.6 1.0 %copy-start.2 = (bf16[4,512,128]{2,1,0:T(8,128)(2,1)S(1)}, bf16[4,512,128]{2,1,0:T(8,128)(2,1)}, u32[]{:S(2)}) copy-start(bf16[4,512,128]{2,1,0:T(8,128)(2,1)} %diag.1) | copy-start | bytes 1572868
  6.7 0.9 %copy-start.3 = (bf16[4,128,128]{2,1,0:T(8,128)(2,1)S(1)}, bf16[4,128,128]{2,1,0:T(8,128)(2,1)}, u32[]{:S(2)}) copy-start(bf16[4,128,128]{2,1,0:T(8,128)(2,1)} %bases.1) | copy-start | bytes 393220
  10.8 7.4 %copy-start.7 = (f32[4,128]{1,0:T(4,128)S(1)}, f32[4,128]{1,0:T(4,128)}, u32[]{:S(2)}) copy-start(f32[4,128]{1,0:T(4,128)} %param.10) | copy-start | bytes 6148
  10.8 1.6 %collective-permute-start.2 = (bf16[2,4,128,128]{3,2,1,0:T(8,128)(2,1)S(1)}, bf16[2,4,128,128]{3,2,1,0:T(8,128)(2,1)S(1)}, u32[]{:S(2)}, u32[]{:S(2)}) collective-permute-start(bf16[2,4,128,128]{3,2,1,0:T(8,128)(2,1)S(1)} %get-tuple-element.23), channel_id=1, source_target_pairs={{0,1},{1,0},{2,3},{3,2},{4,5},{5,4},{6,7},{7,6},{8,9},{9,8},{10,11... | collective-permute-start | bytes 786440 | tf_op jit(solution)/shard_map/ppermute | solution.py:33
  12.5 5.7 %collective-permute-start.3 = (bf16[4,128,128]{2,1,0:T(8,128)(2,1)S(1)}, bf16[4,128,128]{2,1,0:T(8,128)(2,1)S(1)}, u32[]{:S(2)}, u32[]{:S(2)}) collective-permute-start(bf16[4,128,128]{2,1,0:T(8,128)(2,1)S(1)} %fusion.8), channel_id=1, source_target_pairs={{0,2},{1,3},{2,0},{3,1},{4,6},{5,7},{6,4},{7,5},{8,10},{9,11},{10,... | collective-permute-start | bytes 393224 | tf_op jit(solution)/shard_map/ppermute | solution.py:33
  18.4 7.9 %collective-permute-start.4 = (bf16[4,128,128]{2,1,0:T(8,128)(2,1)S(1)}, bf16[4,128,128]{2,1,0:T(8,128)(2,1)S(1)}, u32[]{:S(2)}, u32[]{:S(2)}) collective-permute-start(bf16[4,128,128]{2,1,0:T(8,128)(2,1)S(1)} %fusion.7.refs_1_), channel_id=1, source_target_pairs={{0,4},{1,5},{2,6},{3,7},{4,0},{5,1},{6,2},{7,3},{8,12},{9,13},{10,... | collective-permute-start | bytes 393224 | tf_op jit(solution)/shard_map/ppermute | solution.py:49
  21.2 5.1 %collective-permute-start.5 = (bf16[4,128,128]{2,1,0:T(8,128)(2,1)S(1)}, bf16[4,128,128]{2,1,0:T(8,128)(2,1)S(1)}, u32[]{:S(2)}, u32[]{:S(2)}) collective-permute-start(bf16[4,128,128]{2,1,0:T(8,128)(2,1)S(1)} %fusion.7.refs_1_), channel_id=1, source_target_pairs={{0,1},{1,0},{2,3},{3,2},{4,8},{5,9},{6,10},{7,11},{8,4},{9,5},{10,... | collective-permute-start | bytes 393224 | tf_op jit(solution)/shard_map/ppermute | solution.py:50
  27.5 1.6 %collective-permute-start.6 = (bf16[2,4,128,128]{3,2,1,0:T(8,128)(2,1)S(1)}, bf16[2,4,128,128]{3,2,1,0:T(8,128)(2,1)S(1)}, u32[]{:S(2)}, u32[]{:S(2)}) collective-permute-start(bf16[2,4,128,128]{3,2,1,0:T(8,128)(2,1)S(1)} %get-tuple-element.25), channel_id=1, source_target_pairs={{0,1},{1,0},{2,3},{3,2},{4,5},{5,4},{6,7},{7,6},{8,9},{9,8},{10,11... | collective-permute-start | bytes 786440 | tf_op jit(solution)/shard_map/ppermute | solution.py:33
  29.2 5.7 %collective-permute-start.7 = (bf16[4,128,128]{2,1,0:T(8,128)(2,1)S(1)}, bf16[4,128,128]{2,1,0:T(8,128)(2,1)S(1)}, u32[]{:S(2)}, u32[]{:S(2)}) collective-permute-start(bf16[4,128,128]{2,1,0:T(8,128)(2,1)S(1)} %fusion.9), channel_id=1, source_target_pairs={{0,2},{1,3},{2,0},{3,1},{4,6},{5,7},{6,4},{7,5},{8,10},{9,11},{10,... | collective-permute-start | bytes 393224 | tf_op jit(solution)/shard_map/ppermute | solution.py:33
  35.0 13.9 %copy-start.1 = (bf16[4,128,128]{2,1,0:T(8,128)(2,1)}, bf16[4,128,128]{2,1,0:T(8,128)(2,1)S(1)}, u32[]{:S(2)}) copy-start(bf16[4,128,128]{2,1,0:T(8,128)(2,1)S(1)} %fusion.3.refs_1_) | copy-start | bytes 393220
  35.0 5.0 %collective-permute-start.8 = (bf16[4,128,128]{2,1,0:T(8,128)(2,1)S(1)}, bf16[4,128,128]{2,1,0:T(8,128)(2,1)S(1)}, u32[]{:S(2)}, u32[]{:S(2)}) collective-permute-start(bf16[4,128,128]{2,1,0:T(8,128)(2,1)S(1)} %fusion.3.refs_1_), channel_id=1, source_target_pairs={{0,2},{1,3},{2,0},{3,1},{4,6},{5,7},{6,4},{7,5},{8,10},{9,11},{10,... | collective-permute-start | bytes 393224 | tf_op jit(solution)/shard_map/ppermute | solution.py:33
  40.0 2.8 %collective-permute-start.9 = (bf16[2,4,128,128]{3,2,1,0:T(8,128)(2,1)S(1)}, bf16[2,4,128,128]{3,2,1,0:T(8,128)(2,1)S(1)}, u32[]{:S(2)}, u32[]{:S(2)}) collective-permute-start(bf16[2,4,128,128]{3,2,1,0:T(8,128)(2,1)S(1)} %pad_maximum_fusion.1), channel_id=1, source_target_pairs={{0,1},{1,0},{2,3},{3,2},{4,5},{5,4},{6,7},{7,6},{8,9},{9,8},{10,11... | collective-permute-start | bytes 786440 | tf_op jit(solution)/shard_map/ppermute | solution.py:33
  40.1 8.7 %collective-permute-start.10 = (bf16[4,128,128]{2,1,0:T(8,128)(2,1)S(1)}, bf16[4,128,128]{2,1,0:T(8,128)(2,1)S(1)}, u32[]{:S(2)}, u32[]{:S(2)}) collective-permute-start(bf16[4,128,128]{2,1,0:T(8,128)(2,1)S(1)} %fusion.3.refs_1_), channel_id=1, source_target_pairs={{0,4},{1,5},{2,6},{3,7},{4,0},{5,1},{6,2},{7,3},{8,12},{9,13},{10,... | collective-permute-start | bytes 393224 | tf_op jit(solution)/shard_map/ppermute | solution.py:49
  42.7 6.2 %collective-permute-start.11 = (bf16[4,128,128]{2,1,0:T(8,128)(2,1)S(1)}, bf16[4,128,128]{2,1,0:T(8,128)(2,1)S(1)}, u32[]{:S(2)}, u32[]{:S(2)}) collective-permute-start(bf16[4,128,128]{2,1,0:T(8,128)(2,1)S(1)} %fusion.3.refs_1_), channel_id=1, source_target_pairs={{0,1},{1,0},{2,3},{3,2},{4,8},{5,9},{6,10},{7,11},{8,4},{9,5},{10,... | collective-permute-start | bytes 393224 | tf_op jit(solution)/shard_map/ppermute | solution.py:50
  42.8 6.0 %copy-start.5 = (s32[32]{0:T(128)S(1)}, s32[32]{0:T(128)}, u32[]{:S(2)}) copy-start(s32[32]{0:T(128)} %agg.3) | copy-start | bytes 388
  42.9 6.0 %copy-start.6 = (s32[16]{0:T(128)S(1)}, s32[16]{0:T(128)}, u32[]{:S(2)}) copy-start(s32[16]{0:T(128)} %group.3) | copy-start | bytes 196
  49.9 1.4 %collective-permute-start.12 = (bf16[2,8,32,128]{3,2,1,0:T(8,128)(2,1)S(1)}, bf16[2,8,32,128]{3,2,1,0:T(8,128)(2,1)S(1)}, u32[]{:S(2)}, u32[]{:S(2)}) collective-permute-start(bf16[2,8,32,128]{3,2,1,0:T(8,128)(2,1)S(1)} %get-tuple-element.27), channel_id=1, source_target_pairs={{0,1},{1,0},{2,3},{3,2},{4,5},{5,4},{6,7},{7,6},{8,9},{9,8},{10,11... | collective-permute-start | bytes 393224 | tf_op jit(solution)/shard_map/ppermute | solution.py:33
  51.4 4.3 %collective-permute-start.13 = (bf16[8,32,128]{2,1,0:T(8,128)(2,1)S(1)}, bf16[8,32,128]{2,1,0:T(8,128)(2,1)S(1)}, u32[]{:S(2)}, u32[]{:S(2)}) collective-permute-start(bf16[8,32,128]{2,1,0:T(8,128)(2,1)S(1)} %get-tuple-element.36), channel_id=1, source_target_pairs={{0,2},{1,3},{2,0},{3,1},{4,6},{5,7},{6,4},{7,5},{8,10},{9,11},{10,... | collective-permute-start | bytes 196616 | tf_op jit(solution)/shard_map/ppermute | solution.py:33
  53.0 6.7 %collective-permute-start.15 = (bf16[8,32,128]{2,1,0:T(8,128)(2,1)S(1)}, bf16[8,32,128]{2,1,0:T(8,128)(2,1)S(1)}, u32[]{:S(2)}, u32[]{:S(2)}) collective-permute-start(bf16[8,32,128]{2,1,0:T(8,128)(2,1)S(1)} %get-tuple-element.36), channel_id=1, source_target_pairs={{0,6},{1,7},{2,4},{3,5},{4,2},{5,3},{6,0},{7,1},{8,14},{9,15},{10,... | collective-permute-start | bytes 196616 | tf_op jit(solution)/shard_map/ppermute | solution.py:285
  55.4 4.3 %collective-permute-start.14 = (bf16[8,32,128]{2,1,0:T(8,128)(2,1)S(1)}, bf16[8,32,128]{2,1,0:T(8,128)(2,1)S(1)}, u32[]{:S(2)}, u32[]{:S(2)}) collective-permute-start(bf16[8,32,128]{2,1,0:T(8,128)(2,1)S(1)} %get-tuple-element.35), channel_id=1, source_target_pairs={{0,4},{4,0},{8,12},{12,8},{16,20},{20,16},{24,28},{28,24},{1,5},{5... | collective-permute-start | bytes 196616 | tf_op jit(solution)/shard_map/ppermute | solution.py:33
  60.5 5.3 %collective-permute-start.16 = (bf16[10,32,128]{2,1,0:T(8,128)(2,1)S(1)}, bf16[10,32,128]{2,1,0:T(8,128)(2,1)S(1)}, u32[]{:S(2)}, u32[]{:S(2)}) collective-permute-start(bf16[10,32,128]{2,1,0:T(8,128)(2,1)S(1)} %get-tuple-element.30), channel_id=1, source_target_pairs={{0,8},{4,12},{8,0},{12,4},{16,24},{20,28},{24,16},{28,20},{1,9},{5... | collective-permute-start | bytes 245768 | tf_op jit(solution)/shard_map/ppermute | solution.py:33
  62.1 8.5 %collective-permute-start.17 = (bf16[10,32,128]{2,1,0:T(8,128)(2,1)S(1)}, bf16[10,32,128]{2,1,0:T(8,128)(2,1)S(1)}, u32[]{:S(2)}, u32[]{:S(2)}) collective-permute-start(bf16[10,32,128]{2,1,0:T(8,128)(2,1)S(1)} %get-tuple-element.31), channel_id=1, source_target_pairs={{0,16},{4,20},{8,24},{12,28},{16,0},{20,4},{24,8},{28,12},{1,17},{... | collective-permute-start | bytes 245768 | tf_op jit(solution)/shard_map/ppermute | solution.py:33
  64.0 6.6 %collective-permute-start.18 = (bf16[10,32,128]{2,1,0:T(8,128)(2,1)S(1)}, bf16[10,32,128]{2,1,0:T(8,128)(2,1)S(1)}, u32[]{:S(2)}, u32[]{:S(2)}) collective-permute-start(bf16[10,32,128]{2,1,0:T(8,128)(2,1)S(1)} %get-tuple-element.32), channel_id=1, source_target_pairs={{0,24},{4,28},{8,16},{12,20},{16,8},{20,12},{24,0},{28,4},{1,25},{... | collective-permute-start | bytes 245768 | tf_op jit(solution)/shard_map/ppermute | solution.py:33
